TPU v7x, 32 devices: a whole 2x2x4 slice. The times are simulated.
32 devices in a mesh: gx: 4 (over x, core), gy: 4 (over z), gz: 2 (over y).
Axes of the slice: x: 2, y: 2, z: 4, core: 2. Of those that a mesh axis runs over, the one named last changes fastest.
Arguments:
- fine_coef: bfloat16 [256, 512], P(('gx', 'gy', 'gz')), may hold values from -6 to 6
- mid_leaf: bfloat16 [32, 512], P(('gx', 'gy', 'gz')), may hold values from -6 to 6
- mid_child: int32 [32, 8], P(('gx', 'gy', 'gz')), may hold values from 0 to 7, as said below
- mid_parent: int32 [32], P(('gx', 'gy', 'gz')), may hold values from 0 to 31, each once
- mid_refined: int32 [32], P(('gx', 'gy', 'gz')), may hold values 0 or 1
- fine_nbr: int32 [256, 27], P(('gx', 'gy', 'gz')), may hold values from -1 to 255, as said below
- mid_nbr: int32 [32, 27], P(('gx', 'gy', 'gz')), may hold values from -1 to 31, as said below
- coarse_nbr: int32 [4, 27], replicated, may hold values from -1 to 3, as said below
- op_factor: float32 [3, 32, 3, 8, 8], replicated, may hold values from -1 to 1
- term_weight: float32 [32], replicated, may hold values from 0.05 to 1
Outputs:
- fine_out: float32 [256, 512], P(('gx', 'gy', 'gz'))
- mid_out: float32 [32, 512], P(('gx', 'gy', 'gz'))
Inputs may be any that keep to these rules, and one draw needn't show every extreme that they name: `fine_nbr`: column d names the fine box adjacent across displacement (d // 9 - 1, d // 3 % 3 - 1, d % 3 - 1), or -1. Column 13 is the row's own box. Box g lies on device g // 8; the named box's device differs from the row's device along each of gx, gy, gz by 0 or by that component of the displacement. `mid_nbr`: column d names the middle box adjacent across displacement (d // 9 - 1, d // 3 % 3 - 1, d % 3 - 1), or -1. Column 13 is the row's own box. Box g lies on device g; the named box's device differs from the row's device along each of gx, gy, gz by 0 or by that component of the displacement. `coarse_nbr`: column d names the coarse box adjacent across displacement (d // 9 - 1, d // 3 % 3 - 1, d % 3 - 1), or -1. Column 13 is the row's own box. `mid_child`: the 1 row of one device together name each of its 8 local fine slots exactly once. `mid_parent`: each value appears once.
All inputs are finite; a program needn't handle non-finite values. No bound on the sum of `mid_refined` on one device may be relied on, other than what follows from the above.
Results may differ from a plain program's by a relative error of at most 0.006.
Values may be sent and summed in bfloat16 or wider, within the bound.
A program may use at most 64 MiB of HBM per device.

v0:
```python
import math

import jax
import jax.numpy as jnp
import numpy as np
from jax import lax
from jax.experimental import pallas as pl
from jax.experimental.pallas import tpu as pltpu
from jax.sharding import PartitionSpec as P

exact_mode = lax.Precision.HIGHEST


def poly_multiply(left, right):
    result = [0.0] * (len(left) + len(right) - 1)
    for first, left_coef in enumerate(left):
        for second, right_coef in enumerate(right):
            result[first + second] += left_coef * right_coef
    return result


def poly_compose(coeffs, factor, offset):
    result = [0.0]
    power_term = [1.0]
    for coef in coeffs:
        padded = result + [0.0] * (len(power_term) - len(result))
        result = [padded[place] + coef * power_term[place] for place in range(len(power_term))]
        power_term = poly_multiply(power_term, [offset, factor])
    return result


def legendre_table(basis_order):
    polys = [[1.0], [0.0, 1.0]]
    for degree in range(1, basis_order):
        upper = [0.0] + [(2 * degree + 1) * coef for coef in polys[degree]]
        lower = [degree * coef for coef in polys[degree - 1]] + [0.0] * (
            len(upper) - len(polys[degree - 1])
        )
        polys.append([(upper[place] - lower[place]) / (degree + 1) for place in range(len(upper))])
    return [
        [math.sqrt(2 * degree + 1) * coef for coef in poly_compose(polys[degree], 2.0, -1.0)]
        for degree in range(basis_order)
    ]


def two_scale(basis_order):
    shifted = legendre_table(basis_order)
    filters = np.zeros((2, basis_order, basis_order))
    for which_half in range(2):
        for row_at in range(basis_order):
            halved = poly_compose(shifted[row_at], 0.5, 0.5 * which_half)
            for col_at in range(basis_order):
                product = poly_multiply(halved, shifted[col_at])
                total = sum((coef / (place + 1) for place, coef in enumerate(product)))
                filters[which_half, row_at, col_at] = total / math.sqrt(2.0)
    return np.asarray(filters, np.float32)


def compress(children, filters):
    box_count = children.shape[0]
    basis_order = filters.shape[1]
    cube_form = children.reshape(box_count, 2, 2, 2, basis_order, basis_order, basis_order)
    section_one = jnp.einsum("bijlxyz,ipx->bjlpyz", cube_form, filters, precision=exact_mode)
    section_two = jnp.einsum("bjlpyz,jqy->blpqz", section_one, filters, precision=exact_mode)
    section_three = jnp.einsum("blpqz,lrz->bpqr", section_two, filters, precision=exact_mode)
    return section_three.reshape(box_count, basis_order**3)


def prolong(parents, filters):
    box_count = parents.shape[0]
    basis_order = filters.shape[1]
    cube_form = parents.reshape(box_count, basis_order, basis_order, basis_order)
    section_one = jnp.einsum("bpqr,ipx->bixqr", cube_form, filters, precision=exact_mode)
    section_two = jnp.einsum("bixqr,jqy->bijxyr", section_one, filters, precision=exact_mode)
    section_three = jnp.einsum("bijxyr,lrz->bijlxyz", section_two, filters, precision=exact_mode)
    return section_three.reshape(box_count, 8, basis_order**3)


def local_rows(near_ids, per_device):
    size_y = lax.axis_size("gy")
    size_z = lax.axis_size("gz")
    mine_x = lax.axis_index("gx")
    mine_y = lax.axis_index("gy")
    mine_z = lax.axis_index("gz")
    device = near_ids // per_device
    slot_at = near_ids % per_device
    other_x = device // (size_y * size_z)
    other_y = device // size_z % size_y
    other_z = device % size_z
    cell_at = (other_x - mine_x + 1) * 9 + (other_y - mine_y + 1) * 3 + (other_z - mine_z + 1)
    return jnp.where(near_ids >= 0, cell_at * per_device + slot_at, -1)


MESH = pl.DeviceIdType.MESH
AXES = ("gx", "gy", "gz")
CHUNK = 4


def exchange_kernel(sizes, fine_ref, row_ref, halo, rows, own_sem, fs, fr, ms, mr):
    here = [lax.axis_index(axis) for axis in AXES]

    def peer(dim, offset):
        spot = list(here)
        spot[dim] = lax.rem(here[dim] + offset, sizes[dim])
        return tuple(spot)

    barrier = pltpu.get_barrier_semaphore()
    for dim in range(3):
        for offset in range(1, sizes[dim]):
            pl.semaphore_signal(barrier, inc=1, device_id=peer(dim, offset), device_id_type=MESH)
    own = [
        pltpu.make_async_copy(fine_ref, halo.at[1, 1, 1], own_sem.at[0]),
        pltpu.make_async_copy(row_ref, rows.at[here[0], here[1], here[2]], own_sem.at[1]),
    ]
    for copy in own:
        copy.start()
    for copy in own:
        copy.wait()
    pl.semaphore_wait(barrier, sum(sizes) - 3)
    views = (
        lambda k: halo.at[k],
        lambda k: halo.at[1, k],
        lambda k: halo.at[1, 1, k],
    )
    mine = (
        rows.at[here[0]],
        rows.at[here[0], here[1]],
        rows.at[here[0], here[1], here[2]],
    )
    for dim in (2, 1, 0):
        copies = []
        for side, (offset, land) in enumerate(((1, 0), (sizes[dim] - 1, 2))):
            copies.append(
                pltpu.make_async_remote_copy(
                    src_ref=views[dim](1),
                    dst_ref=views[dim](land),
                    send_sem=fs.at[dim, side],
                    recv_sem=fr.at[dim, side],
                    device_id=peer(dim, offset),
                    device_id_type=MESH,
                )
            )
        for offset in range(1, sizes[dim]):
            copies.append(
                pltpu.make_async_remote_copy(
                    src_ref=mine[dim],
                    dst_ref=mine[dim],
                    send_sem=ms.at[dim, offset],
                    recv_sem=mr.at[dim, offset],
                    device_id=peer(dim, offset),
                    device_id_type=MESH,
                )
            )
        for copy in copies:
            copy.start()
        for copy in copies:
            copy.wait()


def exchange(fine_detail, row):
    sizes = tuple(lax.axis_size(axis) for axis in AXES)
    most = max(sizes)
    vmem = pl.BlockSpec(memory_space=pltpu.VMEM)
    dma = pltpu.SemaphoreType.DMA
    return pl.pallas_call(
        lambda *refs: exchange_kernel(sizes, *refs),
        out_shape=(
            jax.ShapeDtypeStruct((3, 3, 3) + fine_detail.shape, fine_detail.dtype),
            jax.ShapeDtypeStruct(sizes + row.shape, row.dtype),
        ),
        in_specs=[vmem, vmem],
        out_specs=(vmem, vmem),
        scratch_shapes=[dma((2,)), dma((3, 2)), dma((3, 2)), dma((3, most)), dma((3, most))],
        compiler_params=pltpu.CompilerParams(collective_id=0, has_side_effects=True),
        name="exchange",
    )(fine_detail, row)


def apply_kernel(right_ref, weight_ref, mix_ref, wide_ref, tall_ref, live_ref, child_ref, octant_ref, *refs):
    levels = mix_ref.shape[0]
    chunks, terms = right_ref.shape[1], mix_ref.shape[2]
    lanes = CHUNK * 64
    sources, (fine_ref, mid_ref), sums = refs[:levels], refs[levels : levels + 2], refs[levels + 2 :]
    applied = []
    pair = lax.broadcasted_iota(jnp.int32, (CHUNK * 8, lanes), 0)
    lane = lax.broadcasted_iota(jnp.int32, (CHUNK * 8, lanes), 1)
    same_term = pair // 8 == lane // 64
    outer = (same_term & (pair % 8 == lane // 8 % 8)).astype(jnp.float32)
    inner = (same_term & (pair % 8 == lane % 8)).astype(jnp.float32)
    term = lax.broadcasted_iota(jnp.int32, (terms, lanes), 0)
    term_lane = lax.broadcasted_iota(jnp.int32, (terms, lanes), 1) // 64
    for level in range(levels):
        total = sums[level]
        boxes = total.shape[1]
        total[...] = jnp.zeros_like(total)

        def step(c, carry, level=level, total=total, boxes=boxes):
            left = jnp.dot(right_ref[level, c] * weight_ref[c], outer, precision=exact_mode,
                           preferred_element_type=jnp.float32)
            right = jnp.dot(right_ref[level, c], inner, precision=exact_mode,
                            preferred_element_type=jnp.float32)
            pick = (term == term_lane + c * CHUNK).astype(jnp.float32).astype(jnp.bfloat16)
            mix = jnp.dot(mix_ref[level], pick, preferred_element_type=jnp.float32)
            blocks = []
            for ey in range(3):
                for ez in range(3):
                    block = (left[ey * 8 : ey * 8 + 8][:, None, :]
                             * right[ez * 8 : ez * 8 + 8][None, :, :])
                    blocks.append(block.reshape(64, lanes).astype(jnp.bfloat16))
            table = jnp.concatenate(blocks, axis=0)
            spread = jnp.dot(sources[level][...], table, preferred_element_type=jnp.float32)
            spread = spread.reshape(boxes, 3, 8, lanes)
            for a in range(8):
                factor = mix[a * 24 : a * 24 + 24].reshape(3, 8, lanes)
                total[a] += jnp.sum(spread * factor[None], axis=1)
            return carry

        lax.fori_loop(0, chunks, step, 0)
        planes = []
        for a in range(8):
            folded = jnp.sum(total[a], axis=1)
            result = folded[:, :64]
            for k in range(1, CHUNK):
                result = result + folded[:, k * 64 : k * 64 + 64]
            planes.append(result)
        applied.append(jnp.stack(planes, axis=1))

    def children(block):
        wide = jnp.dot(block, wide_ref[...], precision=exact_mode,
                       preferred_element_type=jnp.float32)
        tall = jnp.dot(tall_ref[...], wide, precision=exact_mode,
                       preferred_element_type=jnp.float32)
        return [
            tall[o // 4 * 8 : o // 4 * 8 + 8, o % 4 * 64 : o % 4 * 64 + 64] for o in range(8)
        ]

    fine_direct, mid_direct, parent_out = applied
    slots, mids = fine_direct.shape[0], mid_direct.shape[0]
    totals = [fine_direct[slot] for slot in range(slots)]
    for m in range(mids):
        mid_out = mid_direct[m]
        for o, block in enumerate(children(parent_out[m])):
            mid_out = mid_out + octant_ref[m, o] * block
        mid_ref[m] = mid_out
        for o, block in enumerate(children(mid_out)):
            for slot in range(slots):
                totals[slot] = totals[slot] + child_ref[m * 8 + o, slot] * block
    for slot in range(slots):
        fine_ref[slot] = live_ref[0, slot] * totals[slot]


def apply_levels(factors, weights, sources, live_mask, child_hot, octant_hot, filters):
    levels, terms = factors.shape[:2]
    chunks = terms // CHUNK
    right = jnp.transpose(
        factors.reshape(levels, chunks, CHUNK, 3, 8, 8), (0, 1, 3, 5, 2, 4)
    ).reshape(levels, chunks, 24, CHUNK * 8)
    weight_rows = jnp.repeat(weights, 8).reshape(chunks, 1, CHUNK * 8)
    mix = jnp.transpose(factors.astype(jnp.bfloat16), (0, 3, 2, 4, 1)).reshape(
        levels, 192, terms
    )
    wide = np.einsum("jqy,lrz->qrjlyz", filters, filters).reshape(64, 256)
    tall = np.einsum("ipx->ixp", filters).reshape(16, 8)
    counts = [source.shape[0] // 24 for source in sources]
    vmem = pl.BlockSpec(memory_space=pltpu.VMEM)
    smem = pl.BlockSpec(memory_space=pltpu.SMEM)
    outs = pl.pallas_call(
        apply_kernel,
        out_shape=tuple(jax.ShapeDtypeStruct((n, 8, 64), jnp.float32) for n in counts[:2]),
        in_specs=[vmem] * 5 + [smem] * 3 + [vmem] * levels,
        out_specs=(vmem, vmem),
        scratch_shapes=[pltpu.VMEM((8, n, 8, CHUNK * 64), jnp.float32) for n in counts],
        name="apply_levels",
    )(
        right,
        weight_rows,
        mix,
        jnp.asarray(wide),
        jnp.asarray(tall),
        live_mask[None, :],
        child_hot.reshape(-1, child_hot.shape[-1]),
        octant_hot,
        *sources,
    )
    return tuple(out.reshape(-1, 512) for out in outs)


def pick_sources(table, ids):
    boxes = ids.shape[0]
    picked = table[jnp.maximum(ids, 0)] * (ids >= 0)[:, :, None].astype(jnp.bfloat16)
    picked = picked.reshape(boxes, 3, 9, 8, 64)
    return jnp.transpose(picked, (0, 1, 3, 2, 4)).reshape(boxes * 24, 576)


def shards(
    fine_coef,
    mid_leaf,
    mid_child,
    mid_parent,
    mid_refined,
    fine_nbr,
    mid_nbr,
    coarse_nbr,
    op_factor,
    term_weight,
):
    basis_order = op_factor.shape[-1]
    filters = two_scale(basis_order)
    mid_local = mid_child.shape[0]
    slots_dev = fine_coef.shape[0]
    coarse_count = coarse_nbr.shape[0]
    child_hot = (
        mid_child[:, :, None] == jnp.arange(slots_dev, dtype=jnp.int32)[None, None, :]
    ).astype(jnp.float32)
    refined = mid_refined.astype(jnp.float32)
    live_mask = jnp.sum(child_hot * refined[:, None, None], axis=(0, 1))
    children = fine_coef[mid_child].astype(jnp.float32)
    compressed = compress(children, filters)
    mid_source = jnp.where(
        mid_refined[:, None] > 0, compressed, mid_leaf.astype(jnp.float32)
    ).astype(jnp.bfloat16)
    mid_float = mid_source.astype(jnp.float32)
    spread = prolong(mid_float, filters)
    fine_from = jnp.einsum("mos,mok->sk", child_hot, spread, precision=exact_mode)
    fine_detail = (live_mask[:, None] * (fine_coef.astype(jnp.float32) - fine_from)).astype(
        jnp.bfloat16
    )
    parent = mid_parent // 8
    octant = mid_parent % 8
    place = jnp.stack([parent, octant], axis=1).astype(jnp.bfloat16)
    row = jnp.concatenate(
        [mid_source, jnp.pad(place, ((0, 0), (0, 510)))], axis=1
    ).reshape(mid_local, 8, 128)
    halo, rows = exchange(fine_detail, row)
    rows = rows.reshape(-1, 1024)
    mid_all = rows[:, :512]
    place_all = rows[:, 512:514].astype(jnp.int32)
    parent_all = place_all[:, 0] * 8 + place_all[:, 1]
    slot_hot = (
        jnp.arange(coarse_count * 8, dtype=jnp.int32)[:, None] == parent_all[None, :]
    ).astype(jnp.bfloat16)
    slots = jnp.dot(slot_hot, mid_all, preferred_element_type=jnp.float32)
    coarse_source = compress(slots.reshape(coarse_count, 8, 512), filters)
    from_coarse = prolong(coarse_source, filters).reshape(coarse_count * 8, 512)
    mid_table = (slots - from_coarse).astype(jnp.bfloat16)
    coarse_table = coarse_source.astype(jnp.bfloat16)
    fine_picked = pick_sources(halo.reshape(-1, 512), local_rows(fine_nbr, slots_dev))
    near_slot = jnp.where(mid_nbr >= 0, parent_all[jnp.maximum(mid_nbr, 0)], -1)
    mid_picked = pick_sources(mid_table, near_slot)
    coarse_picked = pick_sources(coarse_table, coarse_nbr[parent])
    octant_hot = (octant[:, None] == jnp.arange(8, dtype=jnp.int32)[None, :]).astype(jnp.float32)
    return apply_levels(
        op_factor,
        term_weight,
        [fine_picked, mid_picked, coarse_picked],
        live_mask,
        child_hot,
        octant_hot,
        filters,
    )


def solution(mesh):
    return jax.shard_map(
        shards,
        mesh=mesh,
        in_specs=(
            P(("gx", "gy", "gz"), None),
            P(("gx", "gy", "gz"), None),
            P(("gx", "gy", "gz"), None),
            P(("gx", "gy", "gz")),
            P(("gx", "gy", "gz")),
            P(("gx", "gy", "gz"), None),
            P(("gx", "gy", "gz"), None),
            P(),
            P(),
            P(),
        ),
        out_specs=(P(("gx", "gy", "gz"), None), P(("gx", "gy", "gz"), None)),
        check_vma=False,
    )
```

profile of v0, /device:TPU:0, one launch (start us, length us, event | category | flops | bytes accessed | tf_op | source)
XLA Modules:
  0.0 67.2 jit_solution(8102045365840803844)
XLA Ops:
  0.6 0.0 copy-start.7
  1.4 0.1 fusion.41
  2.1 0.7 fusion.45
  2.8 1.3 %gather_fusion = bf16[8,512]{1,0:T(8,128)(2,1)S(1)} fusion(bf16[8,512]{1,0:T(8,128)(2,1)} %param.24, s32[1024]{0:T(1024)S(1)} %pad_clamp_fusion.4), kind=kCustom, calls=%fused_computation | custom fusion | bytes 16416 | tf_op jit(solution)/shard_map/gather | solution.py:317
  4.0 0.2 reshape.364
  4.2 1.0 %convolution_bitcast_fusion.6 = f32[2,2,8,8,8]{4,2,3,1,0:T(8,128)S(1)} fusion(f32[2,8,8,1,1,1]{2,1,0,5,4,3:T(8,128)} %constant.173, bf16[2,2,2,8,8,8]{5,4,3,2,1,0:T(8,128)(2,1)S(1)} %reshape.364), kind=kOutput, calls=%fused_computation.11 | convolution fusion | flops 393216 | bytes 16896 | tf_op jit(solution)/shard_map/bijlxyz,ipx->bjlpyz/dot_general | solution.py:63
  5.2 1.0 %convolution_bitcast_fusion.8 = f32[2,8,8,8]{3,2,1,0:T(8,128)S(1)} fusion(f32[2,8,8,1,1]{2,1,0,4,3:T(8,128)} %constant.172, f32[2,2,8,8,8]{4,2,3,1,0:T(8,128)S(1)} %convolution_bitcast_fusion.6), kind=kOutput, calls=%fused_computation.13 | convolution fusion | flops 196608 | bytes 12800 | tf_op jit(solution)/shard_map/bjlpyz,jqy->blpqz/dot_general | solution.py:64
  6.2 0.9 %convolution_bitcast_fusion.9 = bf16[8,8,8]{2,1,0:T(8,128)(2,1)S(1)} fusion(f32[2,8,8,8]{3,2,1,0:T(8,128)S(1)} %convolution_bitcast_fusion.8, f32[2,8,8,1]{2,1,3,0:T(8,128)} %constant.171), kind=kOutput, calls=%fused_computation.14 | convolution fusion | flops 98304 | bytes 5632 | tf_op jit(solution)/shard_map/blpqz,lrz->bpqr/dot_general | solution.py:65
  7.1 0.1 reshape.367
  7.2 0.7 %fusion.47 = (bf16[512]{0:T(512)(128)(2,1)S(1)}, bf16[1,512]{1,0:T(2,128)(2,1)S(1)}) fusion(bf16[1,512]{1,0:T(2,128)(2,1)S(1)} %reshape.367, bf16[1,512]{1,0:T(2,128)(2,1)} %param.25, pred[]{:T(512)} %bitcast.12), kind=kLoop, calls=%fused_computation.112 | loop fusion | flops 1024 | bytes 4097 | tf_op jit(solution)/shard_map/convert_element_type | solution.py:321
  7.9 0.6 maximum_reduce_fusion
  8.5 0.7 %select_reduce_fusion = f32[8]{0:T(128)S(1)} fusion(f32[]{:T(128)} %bitcast.5, s32[8]{0:T(128)} %bitcast.168), kind=kLoop, calls=%fused_computation.86 | loop fusion | flops 184 | bytes 68 | tf_op jit(solution)/shard_map/reduce_sum | solution.py:316
  9.2 0.1 reshape.368
  9.3 0.9 %fusion.15 = f32[2,8,8,8]{3,1,2,0:T(8,128)S(1)} fusion(f32[2,8,8,1]{2,1,3,0:T(8,128)} %constant.171, bf16[8,8,8]{2,1,0:T(8,128)(2,1)S(1)} %reshape.368), kind=kOutput, calls=%fused_computation.38 | convolution fusion | flops 98304 | bytes 5632 | tf_op jit(solution)/shard_map/bpqr,ipx->bixqr/dot_general | solution.py:73
  10.2 1.0 %convolution_bitcast_fusion.7 = f32[2,2,8,8,8]{4,3,2,0,1:T(8,128)S(1)} fusion(f32[2,8,8,1,1]{2,1,4,3,0:T(8,128)} %constant.170, f32[2,8,8,8]{3,1,2,0:T(8,128)S(1)} %fusion.15), kind=kOutput, calls=%fused_computation.12 | convolution fusion | flops 196608 | bytes 12800 | tf_op jit(solution)/shard_map/bixqr,jqy->bijxyr/dot_general | solution.py:74
  11.3 1.9 %convolution_bitcast_fusion.5 = f32[1,2,2,2,8,8,8]{5,6,4,2,1,3,0:T(8,128)S(1)} fusion(f32[2,8,8,1,1,1]{2,1,5,4,3,0:T(8,128)S(1)} %copy-done.7, f32[2,2,8,8,8]{4,3,2,0,1:T(8,128)S(1)} %convolution_bitcast_fusion.7), kind=kOutput, calls=%fused_computation.10 | convolution fusion | flops 393216 | bytes 25088 | tf_op jit(solution)/shard_map/bijxyr,lrz->bijlxyz/dot_general | solution.py:75
  13.1 0.1 copy.65
  13.3 0.2 reshape.370
  13.4 0.9 %fusion.1.refs_0_ = bf16[8,512]{1,0:T(8,128)(2,1)} fusion(f32[8,512]{1,0:T(8,128)S(1)} %reshape.370, bf16[8,512]{1,0:T(8,128)(2,1)S(1)} %copy-done.2, f32[8]{0:T(128)S(1)} %select_reduce_fusion, s32[8]{0:T(128)S(1)} %bitcast.169), kind=kOutput, calls=%fused_computation.17 | convolution fusion | flops 409664 | bytes 32832 | tf_op jit(solution)/shard_map/mos,mok->sk/dot_general | solution.py:324
  14.3 16.8 %exchange.1 = (bf16[3,3,3,8,512]{4,3,2,1,0:T(8,128)(2,1)}, bf16[4,4,2,1,8,128]{5,4,3,2,1,0:T(8,128)(2,1)}) custom-call(bf16[8,512]{1,0:T(8,128)(2,1)} %fusion.1.refs_0_, bf16[1,8,128]{2,1,0:T(8,128)(2,1)} %bitcast.166), custom_call_target="tpu_custom_call" | custom-call | tf_op jit(solution)/shard_map/exchange/pallas_call | solution.py:165
  31.1 0.9 %copy.139 = bf16[4,8,8,128]{3,1,2,0:T(8,128)(2,1)S(1)} copy(bf16[4,8,8,128]{3,2,1,0:T(8,128)(2,1)} %bitcast.165) | data formatting | bytes 131072
  32.0 0.1 copy.107
  32.1 0.1 fusion.13
  32.2 0.6 reshape_reshape.7
  32.8 1.8 %convolution_bitcast_fusion.2 = f32[4,2,2,8,8,8]{3,5,4,2,1,0:T(8,128)S(1)} fusion(f32[2,8,8,1,1,1,1]{2,1,0,6,5,4,3:T(8,128)S(1)} %copy-done.4, f32[4,2,2,2,8,8,8]{6,5,4,3,2,1,0:T(8,128)S(1)} %reshape_reshape.7), kind=kOutput, calls=%fused_computation.7 | convolution fusion | flops 1572864 | bytes 98816 | tf_op jit(solution)/shard_map/bijlxyz,ipx->bjlpyz/dot_general | solution.py:63
  34.7 0.5 copy.69
  35.2 0.5 convolution_bitcast_fusion.3
  35.8 0.6 bitcast_convert_fusion
  36.4 0.4 convolution_bitcast_fusion.4
  36.8 0.2 copy.92
  37.0 0.5 convolution_bitcast_fusion.1
  37.6 1.0 %convolution_bitcast_fusion = f32[4,2,2,2,8,8,8]{6,5,3,4,2,1,0:T(8,128)S(1)} fusion(f32[4,2,2,8,8,8,1]{4,5,6,3,2,1,0:T(8,128)S(1)} %convolution_bitcast_fusion.1, f32[2,8,8,1,1,1,1]{2,1,0,6,5,4,3:T(8,128)S(1)} %copy-done.4), kind=kOutput, calls=%fused_computation.5 | convolution fusion | flops 1572864 | bytes 98816 | tf_op jit(solution)/shard_map/bijxyr,lrz->bijlxyz/dot_general | solution.py:75
  38.6 0.1 copy.74
  38.7 0.5 reshape_reshape.8
  39.3 0.7 %gather_fusion.2 = s32[27]{0:T(128)S(1)} fusion(s32[32]{0:T(128)S(1)} %add_bitcast_fusion, s32[1024]{0:T(1024)S(1)} %pad_clamp_fusion.2), kind=kCustom, calls=%fused_computation.2 | custom fusion | bytes 324 | tf_op jit(solution)/shard_map/gather | solution.py:348
  40.1 0.6 gather_fusion.3
  40.7 0.1 gather.29
  40.8 0.1 reshape.399
  40.9 0.1 fusion.10
  41.0 0.7 %reshape.375.refs_1_ = bf16[24,576]{1,0:T(8,128)(2,1)} reshape(bf16[1,3,8,9,64]{4,3,2,1,0:T(8,128)(2,1)S(1)} %fusion.10) | data formatting | bytes 55296 | tf_op jit(solution)/shard_map/reshape | solution.py:292
  41.7 0.1 convert_element_type.90
  41.9 0.6 gather_fusion.4
  42.5 0.1 gather.32
  42.6 0.1 reshape.400
  42.7 0.1 fusion.9
  42.8 0.7 %reshape.376.refs_2_ = bf16[24,576]{1,0:T(8,128)(2,1)} reshape(bf16[1,3,8,9,64]{4,3,2,1,0:T(8,128)(2,1)S(1)} %fusion.9) | data formatting | bytes 55296 | tf_op jit(solution)/shard_map/reshape | solution.py:292
  43.5 0.1 reshape.412
  43.6 1.1 %gather_fusion.1 = bf16[216,512]{1,0:T(8,128)(2,1)S(1)} fusion(bf16[216,512]{1,0:T(8,128)(2,1)S(1)} %bitcast.159, s32[1024]{0:T(1024)S(1)} %pad_clamp_fusion.3), kind=kCustom, calls=%fused_computation.1 | custom fusion | bytes 443232 | tf_op jit(solution)/shard_map/gather | solution.py:290
  44.7 0.2 gather.26
  44.9 0.1 reshape.398
  45.0 0.1 fusion.3
  45.2 1.1 %reshape.373.refs_0_ = bf16[192,576]{1,0:T(8,128)(2,1)} reshape(bf16[8,3,8,9,64]{4,3,2,1,0:T(8,128)(2,1)S(1)} %fusion.3) | data formatting | bytes 442368 | tf_op jit(solution)/shard_map/reshape | solution.py:292
  46.3 0.5 compare_convert_fusion.3.octant_ref
  46.8 0.7 fusion.34.child_ref
  47.4 0.4 copy.54
  47.9 0.6 copy.55
  48.5 1.2 %reshape.362.right_ref = f32[3,8,24,32]{3,2,1,0:T(8,128)} reshape(f32[3,8,3,8,4,8]{5,4,3,2,1,0:T(4,128)S(1)} %copy.55) | data formatting | bytes 147456 | tf_op jit(solution)/shard_map/reshape | solution.py:257
  49.8 0.7 copy.56
  50.5 0.1 broadcast_in_dim.54
  50.5 0.1 broadcast_in_dim.55
  50.6 0.7 %broadcast_in_dim.56.weight_ref = f32[8,1,32]{2,1,0:T(1,128)} reshape(f32[8,4,8]{2,1,0:T(4,128)S(1)} %broadcast_in_dim.55) | data formatting | bytes 2048 | tf_op jit(solution)/shard_map/broadcast_in_dim | solution.py:258
  51.3 13.1 %apply_levels.1 = (f32[8,8,64]{2,1,0:T(8,128)}, f32[1,8,64]{2,1,0:T(8,128)}) custom-call(f32[3,8,24,32]{3,2,1,0:T(8,128)} %reshape.362.right_ref, f32[8,1,32]{2,1,0:T(1,128)} %broadcast_in_dim.56.weight_ref, bf16[3,192,32]{2,1,0:T(8,128)(2,1)} %bitcast.161, f32[64,256]{1,0:T(8,128)} %constant.139.clone.wide_ref, f32[16,8]{1,0:T(8,128)} %constant.140.clone.tall_ref, ...), custom_call_target="tpu_custom_call" | custom-call | tf_op jit(solution)/shard_map/apply_levels/pallas_call | solution.py:267
  64.4 1.4 %reshape.377 = f32[8,512]{1,0:T(8,128)} reshape(f32[8,8,64]{2,1,0:T(8,128)} %get-tuple-element.8) | data formatting | bytes 32768 | tf_op jit(solution)/shard_map/reshape | solution.py:285
  65.8 1.3 %reshape.378 = f32[1,512]{1,0:T(1,128)} reshape(f32[1,8,64]{2,1,0:T(8,128)} %get-tuple-element.9) | data formatting | bytes 4096 | tf_op jit(solution)/shard_map/reshape | solution.py:285
  (43 shorter events, 0.3 us)
Async XLA Ops:
  0.6 10.6 %copy-start.7 = (f32[2,8,8,1,1,1]{2,1,5,4,3,0:T(8,128)S(1)}, f32[2,8,8,1,1,1]{2,1,5,4,3,0:T(8,128)}, u32[]{:S(2)}) copy-start(f32[2,8,8,1,1,1]{2,1,5,4,3,0:T(8,128)} %constant.169) | copy-start | bytes 1540
  1.3 12.1 %copy-start.2 = (bf16[8,512]{1,0:T(8,128)(2,1)S(1)}, bf16[8,512]{1,0:T(8,128)(2,1)}, u32[]{:S(2)}) copy-start(bf16[8,512]{1,0:T(8,128)(2,1)} %param.24) | copy-start | bytes 24580
  1.4 12.1 %copy-start.10 = (s32[1,8]{1,0:T(1,128)S(1)}, s32[1,8]{1,0:T(1,128)}, u32[]{:S(2)}) copy-start(s32[1,8]{1,0:T(1,128)} %param.26) | copy-start | bytes 100
  9.2 23.6 %copy-start.9 = (f32[8]{0:T(128)}, f32[8]{0:T(128)S(1)}, u32[]{:S(2)}) copy-start(f32[8]{0:T(128)S(1)} %select_reduce_fusion) | copy-start | bytes 100
  13.1 19.7 %copy-start.4 = (f32[2,8,8,1,1,1,1]{2,1,0,6,5,4,3:T(8,128)S(1)}, f32[2,8,8,1,1,1,1]{2,1,0,6,5,4,3:T(8,128)}, u32[]{:S(2)}) copy-start(f32[2,8,8,1,1,1,1]{2,1,0,6,5,4,3:T(8,128)} %constant.174) | copy-start | bytes 1540
  32.8 2.4 %copy-start.6 = (f32[2,8,8,1,1,1]{2,1,0,4,5,3:T(8,128)S(1)}, f32[2,8,8,1,1,1]{2,1,0,4,5,3:T(8,128)}, u32[]{:S(2)}) copy-start(f32[2,8,8,1,1,1]{2,1,0,4,5,3:T(8,128)} %constant.175) | copy-start | bytes 1540
  34.7 1.1 %copy-start.3 = (f32[2,8,8,1,1]{2,1,0,4,3:T(8,128)S(1)}, f32[2,8,8,1,1]{2,1,0,4,3:T(8,128)}, u32[]{:S(2)}) copy-start(f32[2,8,8,1,1]{2,1,0,4,3:T(8,128)} %constant.172) | copy-start | bytes 1540
  35.2 1.8 %copy-start.5 = (f32[2,8,8,1,1,1]{2,1,5,0,4,3:T(8,128)S(1)}, f32[2,8,8,1,1,1]{2,1,5,0,4,3:T(8,128)}, u32[]{:S(2)}) copy-start(f32[2,8,8,1,1,1]{2,1,5,0,4,3:T(8,128)} %constant.176) | copy-start | bytes 1540
  38.6 0.7 %copy-start.12 = (s32[1,27]{1,0:T(1,128)S(1)}, s32[1,27]{1,0:T(1,128)}, u32[]{:S(2)}) copy-start(s32[1,27]{1,0:T(1,128)} %param.30) | copy-start | bytes 328
  38.7 2.0 %copy-start.13 = (s32[4,27]{1,0:T(4,128)S(1)}, s32[4,27]{1,0:T(4,128)}, u32[]{:S(2)}) copy-start(s32[4,27]{1,0:T(4,128)} %param.31) | copy-start | bytes 1300
  39.3 4.2 %copy-start.8 = (s32[8,27]{1,0:T(8,128)S(1)}, s32[8,27]{1,0:T(8,128)}, u32[]{:S(2)}) copy-start(s32[8,27]{1,0:T(8,128)} %param.29) | copy-start | bytes 2596
  39.3 4.4 %copy-start = (bf16[3,3,3,8,512]{4,3,2,1,0:T(8,128)(2,1)S(1)}, bf16[3,3,3,8,512]{4,3,2,1,0:T(8,128)(2,1)}, u32[]{:S(2)}) copy-start(bf16[3,3,3,8,512]{4,3,2,1,0:T(8,128)(2,1)} %get-tuple-element.6) | copy-start | bytes 663556
  44.9 2.5 %copy-start.1 = (f32[3,32,3,8,8]{1,4,3,2,0:T(8,128)S(1)}, f32[3,32,3,8,8]{1,4,3,2,0:T(8,128)}, u32[]{:S(2)}) copy-start(f32[3,32,3,8,8]{1,4,3,2,0:T(8,128)} %param.32) | copy-start | bytes 221188
  48.5 1.9 %copy-start.11 = (f32[32]{0:T(128)S(1)}, f32[32]{0:T(128)}, u32[]{:S(2)}) copy-start(f32[32]{0:T(128)} %param.33) | copy-start | bytes 388
where the time goes:
time: 67.9 us; the launch traced here: 67.2 us
  Pallas kernels  29.9 us (44%)
  local copies, waits for them, and re-layouts  17.9 us (26%)
  matrix products  12.5 us (18%)
  other arithmetic  4.42 us (7%)
  between operations  2.42 us (4%)
    pallas_call x1, Pallas kernels, exchange(): pl.pallas_call(lambda *refs: exchange_kernel(sizes, *refs), out_shape=(ja...  16.8 us
    pallas_call x1, Pallas kernels, apply_levels(): pl.pallas_call(apply_kernel, out_shape=tuple((jax.ShapeDtypeStruct((n, 8,...  13.1 us
    dot_general x2, matrix products, prolong(): jnp.einsum('bijxyr,lrz->bijlxyz', section_two, filters, precision=exact_m...  2.9 us
    dot_general x2, matrix products, compress(): jnp.einsum('bijlxyz,ipx->bjlpyz', cube_form, filters, precision=exact_mode)  2.76 us
    reshape x2, local copies, waits for them, and re-layouts, apply_levels(): return tuple((out.reshape(-1, 512) for out in outs))  2.76 us
    gather x6, local copies, waits for them, and re-layouts, pick_sources(): table[jnp.maximum(ids, 0)] * (ids >= 0)[:, :, None].astype(jnp.bfloat16)  2.74 us
    reshape x3, local copies, waits for them, and re-layouts, pick_sources(): return jnp.transpose(picked, (0, 1, 3, 2, 4)).reshape(boxes * 24, 576)  2.55 us
    dot_general x2, matrix products, prolong(): jnp.einsum('bixqr,jqy->bijxyr', section_one, filters, precision=exact_mode)  1.56 us

commit v1 on v0

v1 whole, which is shorter than its diff:
```python
import math

import jax
import jax.numpy as jnp
import numpy as np
from jax import lax
from jax.experimental import pallas as pl
from jax.experimental.pallas import tpu as pltpu
from jax.sharding import PartitionSpec as P

MESH = pl.DeviceIdType.MESH
AXES = ("gx", "gy", "gz")
CENTRE = 13
QUAD = 4
F32 = jnp.float32
BF16 = jnp.bfloat16


def poly_multiply(left, right):
    result = [0.0] * (len(left) + len(right) - 1)
    for first, left_coef in enumerate(left):
        for second, right_coef in enumerate(right):
            result[first + second] += left_coef * right_coef
    return result


def poly_compose(coeffs, factor, offset):
    result = [0.0]
    power_term = [1.0]
    for coef in coeffs:
        padded = result + [0.0] * (len(power_term) - len(result))
        result = [padded[place] + coef * power_term[place] for place in range(len(power_term))]
        power_term = poly_multiply(power_term, [offset, factor])
    return result


def legendre_table(basis_order):
    polys = [[1.0], [0.0, 1.0]]
    for degree in range(1, basis_order):
        upper = [0.0] + [(2 * degree + 1) * coef for coef in polys[degree]]
        lower = [degree * coef for coef in polys[degree - 1]] + [0.0] * (
            len(upper) - len(polys[degree - 1])
        )
        polys.append([(upper[place] - lower[place]) / (degree + 1) for place in range(len(upper))])
    return [
        [math.sqrt(2 * degree + 1) * coef for coef in poly_compose(polys[degree], 2.0, -1.0)]
        for degree in range(basis_order)
    ]


def two_scale(basis_order):
    shifted = legendre_table(basis_order)
    filters = np.zeros((2, basis_order, basis_order))
    for which_half in range(2):
        for row_at in range(basis_order):
            halved = poly_compose(shifted[row_at], 0.5, 0.5 * which_half)
            for col_at in range(basis_order):
                product = poly_multiply(halved, shifted[col_at])
                total = sum((coef / (place + 1) for place, coef in enumerate(product)))
                filters[which_half, row_at, col_at] = total / math.sqrt(2.0)
    return np.asarray(filters, np.float32)


def halves(array):
    high = array.astype(BF16)
    return high, (array - high.astype(array.dtype)).astype(BF16)


def np_halves(array):
    array = np.asarray(array, np.float32)
    high = array.astype(BF16)
    return high, (array - high.astype(np.float32)).astype(BF16)


def dot(left, right):
    return jnp.dot(left, right, preferred_element_type=F32)


def dot_rows(left, right):
    return lax.dot_general(left, right, (((1,), (1,)), ((), ())), preferred_element_type=F32)


def constants(terms, devices, batch):
    filters = two_scale(8)
    table = {}
    row = np.arange(8 * terms)
    lane = np.arange(64 * terms)
    same = (row % terms)[:, None] == (lane // 64)[None, :]
    spread = [same & ((row // terms)[:, None] == part[None, :]) for part in (lane // 8 % 8, lane % 8)]
    table["spread"] = np.concatenate(spread, axis=1).astype(BF16)
    swap = (row // 8)[:, None] == (row % terms)[None, :]
    swap &= (row % 8)[:, None] == (row // terms)[None, :]
    table["swap"] = swap.astype(BF16)
    table["widen"] = (np.arange(72)[:, None] == (np.arange(192) // 8)[None, :]).astype(BF16)
    plane = np.einsum("jqy,lrz->jlyzqr", filters, filters)
    table["gather_plane"] = np.concatenate(np_halves(plane.reshape(256, 64)), axis=1)
    plane = np.einsum("jqy,lrz->qrjlyz", filters, filters)
    table["scatter_plane"] = np.concatenate(np_halves(plane.reshape(64, 256)), axis=1)
    parts = [np.asarray(part, np.float32) for part in np_halves(filters)]
    both = np.stack(parts, axis=1).reshape(4, 8, 8)
    flip = np.swapaxes(both, 1, 2)
    table["child_in"] = np.repeat(both, 8, axis=2)
    table["child_out"] = np.tile(np.repeat(flip, 8, axis=1), (1, 1, 4))
    table["mid_in"] = np.tile(both, (1, 1, devices))
    table["mid_out"] = np.tile(flip, (1, 1, batch * 4))
    own = [np.concatenate([flip[2 * i], flip[2 * i], flip[2 * i + 1]], axis=1) for i in range(2)]
    table["own_out"] = np.stack(own)
    cell = np.arange(27 * 8) // 8
    cells = np.zeros((8, 27 * 8), np.int32)
    cells[:4] = np.stack([cell // 9 - 1, cell // 3 % 3 - 1, cell % 3 - 1, np.arange(27 * 8) % 8])
    table["cells"] = cells
    return table


def kernel(sizes, names, batch, levels, terms, coarse, args, consts, outs, scratch):
    size_x, size_y, size_z = sizes
    devices = size_x * size_y * size_z
    here = [lax.axis_index(axis) for axis in AXES]
    me = (here[0] * size_y + here[1]) * size_z + here[2]
    fine_ref, mid_ref = outs
    (loaded, held, halo, rows, factor_left, factor_right, tables, mixers, mixers_t, block_mix, picks, coarse_tab,
     load_sem, held_sem, row_send, row_recv, halo_send, halo_recv) = scratch

    def place_of(device):
        return (device // (size_y * size_z), device // size_z % size_y, device % size_z)

    def each_peer(body):
        if devices <= 64:
            for offset in range(1, devices):
                body(lax.rem(me + offset, devices))
        else:
            def step(offset, carry):
                body(lax.rem(me + offset, devices))
                return carry
            lax.fori_loop(1, devices, step, 0)

    barrier = pltpu.get_barrier_semaphore()
    each_peer(lambda peer: pl.semaphore_signal(
        barrier, inc=1, device_id=place_of(peer), device_id_type=MESH))

    loads = {}
    for at, (name, source) in enumerate(args.items()):
        loads[name] = pltpu.make_async_copy(source, loaded[name], load_sem.at[at])
    for at, (name, source) in enumerate(consts.items()):
        loads[name] = pltpu.make_async_copy(source, held[name], held_sem.at[at])
    order = ["mid_child", "mid_parent", "mid_refined", "fine_coef", "mid_leaf", "child_in", "gather_plane",
             "child_out", "scatter_plane"]
    order += [name for name in loads if name not in order]
    for name in order:
        loads[name].start()

    def ready(*wanted):
        for name in wanted:
            loads[name].wait()

    ready("mid_child", "mid_parent", "mid_refined", "fine_coef", "mid_leaf", "child_in", "gather_plane")
    child = [loaded["mid_child"][0, o] for o in range(8)]
    refined = loaded["mid_refined"][0] > 0
    live = jnp.where(refined, 1.0, 0.0).astype(F32)
    mid_parent = loaded["mid_parent"][0]
    my_parent = lax.shift_right_logical(mid_parent, 3)
    my_octant = mid_parent & 7
    flat = loaded["fine_coef"][...].astype(F32)
    by_row = jnp.concatenate([flat[:, 64 * x : 64 * x + 64] for x in range(8)], axis=0)
    slot_lane = lax.broadcasted_iota(jnp.int32, (8, 64), 1) & 7
    child_in = [held["child_in"][k] for k in range(4)]
    blocks = []
    for part in range(2):
        for jl in range(4):
            block = jnp.where(slot_lane == child[jl], child_in[part], 0.0)
            blocks.append(block + jnp.where(slot_lane == child[4 + jl], child_in[2 + part], 0.0))
    mixed = dot(jnp.concatenate(blocks, axis=0).astype(BF16), by_row.astype(BF16))
    mixed = mixed[:32] + mixed[32:]

    def stack_halves(array):
        high, low = halves(array)
        return jnp.concatenate([high.astype(F32), low.astype(F32)], axis=0).astype(BF16)

    def close_children(mixed, boxes):
        wide = [
            jnp.concatenate([mixed[(4 * k + jl) * 8 : (4 * k + jl) * 8 + 8] for jl in range(4)], axis=1)
            for k in range(boxes)
        ]
        wide = wide[0] if boxes == 1 else jnp.concatenate(wide, axis=0)
        got = dot(stack_halves(wide), held["gather_plane"][...])
        count = boxes * 8
        return got[:count, :64] + got[:count, 64:] + got[count:, :64]

    def open_plane(block, exact=False):
        count = block.shape[0]
        if exact:
            got = dot(block.astype(BF16), held["scatter_plane"][...])
            return got[:, :256] + got[:, 256:]
        got = dot(stack_halves(block), held["scatter_plane"][...])
        return got[:count, :256] + got[:count, 256:] + got[count:, :256]

    def lanes_to_rows(plane):
        count = plane.shape[0] // 8
        return jnp.concatenate(
            [plane[8 * k : 8 * k + 8, 64 * jl : 64 * jl + 64] for k in range(count) for jl in range(4)], axis=0
        )

    def triple(rows_f32):
        high, low = halves(rows_f32)
        high, low = high.astype(F32), low.astype(F32)
        return jnp.concatenate([high, low, high], axis=0).astype(BF16)

    compressed = close_children(mixed, 1)
    leaf = jnp.broadcast_to(loaded["mid_leaf"][...].astype(F32), (8, 512))
    block_lane = lax.shift_right_logical(lax.broadcasted_iota(jnp.int32, (8, 512), 1), 6)
    leaf = jnp.where(block_lane == lax.broadcasted_iota(jnp.int32, (8, 512), 0), leaf, 0.0)
    leaf_square = leaf[:, :64]
    for x in range(1, 8):
        leaf_square = leaf_square + leaf[:, 64 * x : 64 * x + 64]
    mid_source = jnp.where(refined, compressed, leaf_square).astype(BF16).astype(F32)
    note = lax.broadcasted_iota(jnp.int32, (8, 64), 1)
    place = jnp.where(note == 0, my_parent + 1, jnp.where(note == 1, my_octant, 0)).astype(F32)
    rows[me] = jnp.concatenate([mid_source, place], axis=1).astype(BF16)

    ready("child_out", "scatter_plane")
    jl_lane = lax.shift_right_logical(lax.broadcasted_iota(jnp.int32, (64, 32), 1), 3)
    slot_row = lax.broadcasted_iota(jnp.int32, (64, 32), 0) & 7

    def child_lane(i):
        return jnp.where(jl_lane == 0, child[4 * i],
                         jnp.where(jl_lane == 1, child[4 * i + 1],
                                   jnp.where(jl_lane == 2, child[4 * i + 2], child[4 * i + 3])))

    chosen = [slot_row == child_lane(i) for i in range(2)]
    out_parts = [
        jnp.where(chosen[0], held["child_out"][part], 0.0)
        + jnp.where(chosen[1], held["child_out"][2 + part], 0.0)
        for part in range(2)
    ]
    child_out = jnp.concatenate([out_parts[0], out_parts[0], out_parts[1]], axis=1).astype(BF16)

    def to_children(plane):
        return dot(child_out, triple(lanes_to_rows(plane)))

    detail = live * (by_row - to_children(open_plane(mid_source, exact=True)))
    detail = jnp.concatenate([detail[8 * x : 8 * x + 8] for x in range(8)], axis=1)
    halo[CENTRE] = detail.astype(BF16)

    steps = [(c // 9 - 1, c // 3 % 3 - 1, c % 3 - 1) for c in range(27)]

    def inside(step):
        tests = []
        for at, size, move in zip(here, sizes, step):
            if move == 1:
                tests.append(at < size - 1)
            elif move == -1:
                tests.append(at > 0)
        found = tests[0]
        for test in tests[1:]:
            found = found & test
        return found

    def halo_copy(cell):
        move = steps[cell]
        peer = tuple(at + part for at, part in zip(here, move))
        return pltpu.make_async_remote_copy(
            src_ref=halo.at[CENTRE],
            dst_ref=halo.at[26 - cell],
            send_sem=halo_send.at[cell],
            recv_sem=halo_recv.at[26 - cell],
            device_id=peer,
            device_id_type=MESH,
        )

    others = [cell for cell in range(27) if cell != CENTRE]
    pl.semaphore_wait(barrier, devices - 1)
    each_peer(lambda peer: pltpu.make_async_remote_copy(
        src_ref=rows.at[me],
        dst_ref=rows.at[me],
        send_sem=row_send.at[0],
        recv_sem=row_recv.at[0],
        device_id=place_of(peer),
        device_id_type=MESH,
    ).start())
    for cell in others:
        @pl.when(inside(steps[cell]))
        def _(cell=cell):
            halo_copy(cell).start()

        @pl.when(jnp.logical_not(inside(steps[cell])))
        def _(cell=cell):
            halo[cell] = jnp.zeros(halo.shape[1:], BF16)

    ready("op_factor", "term_weight", "spread", "swap", "widen")
    factor = loaded["op_factor"]
    planes = []
    for level in range(levels):
        for e in range(3):
            planes.append(jnp.concatenate([factor[level, e, b] for b in range(8)], axis=1))
    plane = jnp.concatenate(planes, axis=0)
    weight = jnp.concatenate([loaded["term_weight"][...]] * 8, axis=1)
    rounded = plane.astype(BF16)
    left_side = stack_halves(plane * weight)
    right_side = stack_halves(plane)
    count = plane.shape[0]
    width = 64 * terms
    for at in range(0, width, 512):
        got = dot(left_side, held["spread"][:, at : at + 512])
        got = got[:count] + got[count:]
        factor_left[:, :, at : at + 512] = got.reshape(levels * 3, 8, 512)
        got = dot(right_side, held["spread"][:, width + at : width + at + 512])
        got = got[:count] + got[count:]
        factor_right[:, :, at : at + 512] = got.reshape(levels * 3, 8, 512)
    turned = dot_rows(held["swap"][...], rounded).astype(BF16)
    mixers[...] = turned
    mixers_t[...] = dot(turned, held["widen"][...])

    def table_step(at, carry):
        level, ey = at // 3, at % 3
        left = factor_left.at[at]
        for ez in range(3):
            right = factor_right[level * 3 + ez]
            base = (ey * 3 + ez) * 64
            for k in range(4):
                pair = [left[2 * k + half : 2 * k + half + 1, :] * right for half in range(2)]
                start = pl.multiple_of(base + 16 * k, 16)
                tables[level, pl.ds(start, 16), :] = jnp.concatenate(pair, axis=0).astype(BF16)
        return carry

    lax.fori_loop(0, levels * 3, table_step, 0)
    own_lane = (lax.broadcasted_iota(jnp.int32, (8, 192), 1) & 7) == lax.broadcasted_iota(jnp.int32, (8, 192), 0)

    def mix_step(at, carry):
        some = mixers_t[pl.ds(pl.multiple_of(at * 16, 16), 16), :]
        some = jnp.where(own_lane[None], jnp.broadcast_to(some[:, None, :], (16, 8, 192)), 0.0)
        block_mix[pl.ds(pl.multiple_of(at * 128, 128), 128), :] = some.reshape(128, 192).astype(BF16)
        return carry

    lax.fori_loop(0, terms // 2, mix_step, 0)

    ready("cells", "fine_nbr")
    cells = held["cells"]
    spot = [here[k] + cells[k : k + 1, :] for k in range(3)]
    there = None
    for k in range(3):
        test = (spot[k] >= 0) & (spot[k] < sizes[k])
        there = test if there is None else there & test
    names_row = ((spot[0] * size_y + spot[1]) * size_z + spot[2]) * 8 + cells[3:4, :]
    names_row = jnp.where(there, names_row, -2)
    near = loaded["fine_nbr"][...]
    hot = [(near[:, d : d + 1] == names_row).astype(F32) for d in range(27)]
    picks[...] = jnp.concatenate(hot, axis=0).astype(BF16)

    ready("mid_in", "mid_out", "own_out", "mid_nbr", "coarse_nbr")
    all_rows = rows.at[pl.ds(0, devices - 1)]
    pltpu.make_async_copy(all_rows, all_rows, row_recv.at[0]).wait()
    gathered = rows[...].astype(F32).reshape(devices * 8, 128).astype(BF16)
    reader_lane = lax.broadcasted_iota(jnp.int32, (8, 128), 1)
    reader = jnp.where(reader_lane == 64, 8.0, jnp.where(reader_lane == 65, 1.0, 0.0)).astype(BF16)
    code = dot_rows(reader, gathered) - 8.0
    near_rows = []
    for d in range(27):
        named = loaded["mid_nbr"][0, d]
        got = rows[jnp.maximum(named, 0)].astype(F32)
        near_rows.append(jnp.where(named >= 0, got, 0.0))
    near_rows = jnp.concatenate(near_rows, axis=0)
    near_code = near_rows[:, 64:65] * 8.0 + near_rows[:, 65:66] - 8.0
    batch_lane = lax.broadcasted_iota(jnp.int32, (8, batch * 32), 1)
    batch_code = lax.shift_right_logical(batch_lane, 5) * 8 + (lax.shift_right_logical(batch_lane, 3) & 3)

    def coarse_step(at, total):
        first = at * (batch * 8)
        first_f = first.astype(F32) if hasattr(first, "astype") else float(first)
        blocks = []
        for part in range(2):
            for k in range(batch):
                for jl in range(4):
                    want = first_f + float(8 * k + jl)
                    block = jnp.where(code == want, held["mid_in"][part], 0.0)
                    blocks.append(block + jnp.where(code == want + 4.0, held["mid_in"][2 + part], 0.0))
        mixed = dot(jnp.concatenate(blocks, axis=0).astype(BF16), gathered)
        half = batch * 32
        source = close_children(mixed[:half, :64] + mixed[half:, :64], batch)
        held_source = source.astype(BF16).astype(F32)
        double = jnp.concatenate([held_source, held_source], axis=1)
        coarse_tab[pl.ds(at * batch, batch)] = double.reshape(batch, 8, 128)
        lane_code = first_f + batch_code.astype(F32)
        parts = [[], []]
        for d in range(27):
            mine = near_code[8 * d : 8 * d + 8]
            lower, upper = mine == lane_code, mine == lane_code + 4.0
            for part in range(2):
                block = jnp.where(lower, held["mid_out"][part], 0.0)
                parts[part].append(block + jnp.where(upper, held["mid_out"][2 + part], 0.0))
        parts = [jnp.concatenate(part, axis=0).astype(BF16) for part in parts]
        spread = triple(lanes_to_rows(open_plane(source)))
        rows_out = dot(jnp.concatenate([parts[0], parts[0], parts[1]], axis=1), spread)
        return total + rows_out

    batches = coarse // batch
    zero = jnp.zeros((216, 64), F32)
    from_coarse = coarse_step(0, zero) if batches == 1 else lax.fori_loop(0, batches, coarse_step, zero)
    mid_detail = near_rows[:, :64] - from_coarse
    mid_blocks = [
        jnp.concatenate([mid_detail[(ex * 9 + e) * 8 : (ex * 9 + e) * 8 + 8] for e in range(9)], axis=1)
        for ex in range(3)
    ]
    low_lane = lax.broadcasted_iota(jnp.int32, (8, 128), 1) < 64
    coarse_blocks = []
    for ex in range(3):
        got = []
        for e in range(9):
            named = loaded["coarse_nbr"][my_parent, ex * 9 + e]
            got.append(jnp.where(named >= 0, coarse_tab[jnp.maximum(named, 0)], 0.0))
        pairs = [jnp.where(low_lane, got[e], got[e + 1]) for e in range(0, 8, 2)] + [got[8][:, :64]]
        coarse_blocks.append(jnp.concatenate(pairs, axis=1))

    def apply_one(level, blocks):
        parts = []
        if level > 0:
            parts.append(jnp.zeros((24 * level, 576), F32))
        parts += blocks
        if level < levels - 1:
            parts.append(jnp.zeros((24 * (levels - 1 - level), 576), F32))
        mixed = dot(mixers[...], jnp.concatenate(parts, axis=0).astype(BF16)).astype(BF16)
        total = None
        for at in range(0, terms // QUAD):
            got = dot(mixed[at * 32 : at * 32 + 32], tables[level, :, at * 256 : at * 256 + 256])
            total = got if total is None else total + got
        result = total[:8, :64]
        for k in range(1, QUAD):
            result = result + total[8 * k : 8 * k + 8, 64 * k : 64 * k + 64]
        return result

    coarse_out = apply_one(2, coarse_blocks)
    mid_direct = apply_one(1, mid_blocks)
    plane = open_plane(coarse_out)
    my_jl = my_octant & 3
    mine = plane[:, :64]
    for jl in range(1, 4):
        mine = jnp.where(my_jl == jl, plane[:, 64 * jl : 64 * jl + 64], mine)
    own_out = jnp.where(my_octant >= 4, held["own_out"][1], held["own_out"][0]).astype(BF16)
    mid_out = mid_direct + dot(own_out, triple(mine))
    for a in range(8):
        mid_ref[0:1, 64 * a : 64 * a + 64] = mid_out[a : a + 1]

    for cell in others:
        @pl.when(inside(steps[cell]))
        def _(cell=cell):
            halo_copy(26 - cell).wait_recv()
    wanted = halo[...].astype(F32).reshape(216, 512).astype(BF16)
    got = dot(picks[...], wanted)
    blocks = []
    for ex in range(3):
        for a in range(8):
            blocks.append(jnp.concatenate(
                [got[(ex * 9 + e) * 8 : (ex * 9 + e) * 8 + 8, 64 * a : 64 * a + 64] for e in range(9)], axis=1))
    sources = jnp.concatenate(blocks, axis=0).astype(BF16)
    total = None
    for at in range(terms // QUAD):
        spread = dot(sources, tables[0, :, at * 256 : at * 256 + 256]).astype(BF16)
        part = dot(block_mix[at * 256 : at * 256 + 256, :], spread)
        total = part if total is None else total + part
    direct = total[:64, :64]
    for k in range(1, QUAD):
        direct = direct + total[64 * k : 64 * k + 64, 64 * k : 64 * k + 64]
    fine = live * (direct + to_children(open_plane(mid_out)))
    fine_ref[...] = jnp.concatenate([fine[8 * x : 8 * x + 8] for x in range(8)], axis=1)

    pltpu.make_async_copy(all_rows, all_rows, row_send.at[0]).wait()
    for cell in others:
        @pl.when(inside(steps[cell]))
        def _(cell=cell):
            halo_copy(cell).wait_send()


SCALARS = ("mid_child", "mid_parent", "mid_refined", "mid_nbr", "coarse_nbr")


def shards(sizes, fine_coef, mid_leaf, mid_child, mid_parent, mid_refined, fine_nbr, mid_nbr, coarse_nbr,
           op_factor, term_weight):
    levels, terms = op_factor.shape[:2]
    coarse = coarse_nbr.shape[0]
    devices = math.prod(sizes)
    batch = math.gcd(coarse, 4)
    assert mid_child.shape == (1, 8) and fine_coef.shape == (8, 512) and terms % QUAD == 0
    args = dict(
        mid_child=mid_child, mid_parent=mid_parent, mid_refined=mid_refined, fine_coef=fine_coef,
        mid_leaf=mid_leaf, fine_nbr=fine_nbr, mid_nbr=mid_nbr, coarse_nbr=coarse_nbr,
        op_factor=jnp.transpose(op_factor, (0, 2, 3, 4, 1)), term_weight=term_weight[None, :],
    )
    consts = {name: jnp.asarray(value) for name, value in constants(terms, devices, batch).items()}
    arg_names, const_names = list(args), list(consts)
    dma = pltpu.SemaphoreType.DMA
    width = 64 * terms

    def buffer(name, value):
        space = pltpu.SMEM if name in SCALARS else pltpu.VMEM
        return space(value.shape, value.dtype)

    scratch = [buffer(name, value) for name, value in args.items()]
    scratch += [buffer(name, value) for name, value in consts.items()]
    scratch += [
        pltpu.VMEM((27, 8, 512), BF16),
        pltpu.VMEM((devices, 8, 128), BF16),
        pltpu.VMEM((levels * 3, 8, width), F32),
        pltpu.VMEM((levels * 3, 8, width), F32),
        pltpu.VMEM((levels, 576, width), BF16),
        pltpu.VMEM((8 * terms, 24 * levels), BF16),
        pltpu.VMEM((8 * terms, 192), F32),
        pltpu.VMEM((64 * terms, 192), BF16),
        pltpu.VMEM((216, 216), BF16),
        pltpu.VMEM((coarse, 8, 128), F32),
        dma((len(args),)), dma((len(consts),)), dma((1,)), dma((1,)), dma((27,)), dma((27,)),
    ]

    def body(*refs):
        n_args, n_consts = len(arg_names), len(const_names)
        ins, refs = refs[: n_args + n_consts], refs[n_args + n_consts :]
        outs, refs = refs[:2], refs[2:]
        loaded = dict(zip(arg_names, refs[:n_args]))
        held = dict(zip(const_names, refs[n_args : n_args + n_consts]))
        kernel(sizes, None, batch, levels, terms, coarse, dict(zip(arg_names, ins[:n_args])),
               dict(zip(const_names, ins[n_args:])), outs, (loaded, held) + tuple(refs[n_args + n_consts :]))

    vmem = pl.BlockSpec(memory_space=pltpu.VMEM)
    hbm = pl.BlockSpec(memory_space=pl.ANY)
    return pl.pallas_call(
        body,
        out_shape=(jax.ShapeDtypeStruct((8, 512), F32), jax.ShapeDtypeStruct((1, 512), F32)),
        in_specs=[hbm] * (len(args) + len(consts)),
        out_specs=(vmem, vmem),
        scratch_shapes=scratch,
        compiler_params=pltpu.CompilerParams(
            collective_id=0, has_side_effects=True, vmem_limit_bytes=58 * 1024 * 1024),
        name="tree",
    )(*args.values(), *consts.values())


def solution(mesh):
    sizes = tuple(mesh.shape[axis] for axis in AXES)
    split = P(AXES, None)
    line = P(AXES)
    return jax.shard_map(
        lambda *args: shards(sizes, *args),
        mesh=mesh,
        in_specs=(split, split, split, line, line, split, split, P(), P(), P()),
        out_specs=(split, split),
        check_vma=False,
    )
```

time: 67.9 us -> 22.6 us (0.33)
  local copies, waits for them, and re-layouts: 17.9 us -> 2.55 us
  matrix products: 12.5 us -> 0 us
  Pallas kernels: 29.9 us -> 17.8 us
  other arithmetic: 4.42 us -> 0 us
    dot_general x14 -> x0, matrix products: 12.5 us -> none  [the longest x2 2.9 us: prolong(): jnp.einsum('bijxyr,lrz->bijlxyz', section_two, filters, precision=exact_m...]
    pallas_call x2 -> x1, Pallas kernels: 29.9 us -> 17.8 us  [shards(): pl.pallas_call(body, out_shape=(jax.ShapeDtypeStruct((8, 512), F32), jax....]
    reshape x7 -> x0, local copies, waits for them, and re-layouts: 6.62 us -> none  [the longest x2 2.76 us: apply_levels(): return tuple((out.reshape(-1, 512) for out in outs))]
    gather x8 -> x0, local copies, waits for them, and re-layouts: 4.7 us -> none  [the longest x6 2.74 us: pick_sources(): table[jnp.maximum(ids, 0)] * (ids >= 0)[:, :, None].astype(jnp.bfloat16)]
    transpose x6 -> x0, local copies, waits for them, and re-layouts: 2.27 us -> none  [the longest x1 0.67 us: apply_levels(): jnp.transpose(factors.astype(jnp.bfloat16), (0, 3, 2, 4, 1))]
    convert_element_type x6 -> x0, other arithmetic: 1.93 us -> none  [the longest x1 0.71 us: shards(): mid_source = jnp.where(mid_refined[:, None] > 0, compressed, mid_leaf.ast...]
    another operation x5 -> x0, local copies, waits for them, and re-layouts: 1.54 us -> none  [the longest x1 0.59 us: compress(): children.reshape(box_count, 2, 2, 2, basis_order, basis_order, basis_order)]
    unnamed x31 -> x2, local copies, waits for them, and re-layouts: 1.46 us -> 2.55 us
where the time goes in v1:
time: 22.6 us; the launch traced here: 22.3 us
  Pallas kernels  17.8 us (79%)
  local copies, waits for them, and re-layouts  2.55 us (11%)
  between operations  1.93 us (9%)
    pallas_call x1, Pallas kernels, shards(): pl.pallas_call(body, out_shape=(jax.ShapeDtypeStruct((8, 512), F32), jax....  17.8 us
    unnamed x2, local copies, waits for them, and re-layouts  2.55 us

profile of v1, /device:TPU:0, one launch (start us, length us, event | category | flops | bytes accessed | tf_op | source)
XLA Modules:
  0.0 22.3 jit_solution(3156357256852472956)
XLA Ops:
  1.9 17.8 %tree.1 = (f32[8,512]{1,0:T(8,128)}, f32[1,512]{1,0:T(1,128)}) custom-call(s32[1,8]{1,0:T(1,128)} %refs_0_.1, s32[1]{0:T(128)S(6)} %copy.25.refs_1_, s32[1]{0:T(128)S(6)} %copy.26.refs_2_, bf16[8,512]{1,0:T(8,128)(2,1)} %refs_3_.1, bf16[1,512]{1,0:T(2,128)(2,1)} %refs_4_.1, s32[8,27]{1,0:T(8,128)} %refs_5_.1, s32[1,27]{1,0:T(1,128)} %refs_6_.1, ...), custom_call_target="tpu_custom_call" | custom-call | tf_op jit(solution)/shard_map/tree/pallas_call | solution.py:523
  19.7 1.3 %copy.27 = f32[8,512]{1,0:T(8,128)} copy(f32[8,512]{1,0:T(8,128)} %get-tuple-element.4) | data formatting | bytes 32768
  21.0 1.2 %copy.28 = f32[1,512]{1,0:T(1,128)} copy(f32[1,512]{1,0:T(1,128)} %get-tuple-element.5) | data formatting | bytes 4096

commit v2 on v1

--- a/solution.py
+++ b/solution.py
@@ -121,22 +121,20 @@
     (loaded, held, halo, rows, factor_left, factor_right, tables, mixers, mixers_t, block_mix, picks, coarse_tab,
      load_sem, held_sem, row_send, row_recv, halo_send, halo_recv) = scratch
 
-    def place_of(device):
-        return (device // (size_y * size_z), device // size_z % size_y, device % size_z)
-
     def each_peer(body):
         if devices <= 64:
-            for offset in range(1, devices):
-                body(lax.rem(me + offset, devices))
+            spots = [
+                [at] + [lax.rem(at + k, size) for k in range(1, size)] for at, size in zip(here, sizes)
+            ]
+            peers = [(x, y, z) for x in spots[0] for y in spots[1] for z in spots[2]]
+            for peer in peers[1:]:
+                body(peer)
         else:
             def step(offset, carry):
-                body(lax.rem(me + offset, devices))
+                device = lax.rem(me + offset, devices)
+                body((device // (size_y * size_z), device // size_z % size_y, device % size_z))
                 return carry
             lax.fori_loop(1, devices, step, 0)
-
-    barrier = pltpu.get_barrier_semaphore()
-    each_peer(lambda peer: pl.semaphore_signal(
-        barrier, inc=1, device_id=place_of(peer), device_id_type=MESH))
 
     loads = {}
     for at, (name, source) in enumerate(args.items()):
@@ -148,6 +146,10 @@
     order += [name for name in loads if name not in order]
     for name in order:
         loads[name].start()
+
+    barrier = pltpu.get_barrier_semaphore()
+    each_peer(lambda peer: pl.semaphore_signal(
+        barrier, inc=1, device_id=peer, device_id_type=MESH))
 
     def ready(*wanted):
         for name in wanted:
@@ -274,9 +276,10 @@
         dst_ref=rows.at[me],
         send_sem=row_send.at[0],
         recv_sem=row_recv.at[0],
-        device_id=place_of(peer),
+        device_id=peer,
         device_id_type=MESH,
     ).start())
+
     for cell in others:
         @pl.when(inside(steps[cell]))
         def _(cell=cell):
@@ -345,6 +348,28 @@
     near = loaded["fine_nbr"][...]
     hot = [(near[:, d : d + 1] == names_row).astype(F32) for d in range(27)]
     picks[...] = jnp.concatenate(hot, axis=0).astype(BF16)
+
+    for cell in others:
+        @pl.when(inside(steps[cell]))
+        def _(cell=cell):
+            halo_copy(26 - cell).wait_recv()
+
+    wanted = halo[...].astype(F32).reshape(216, 512).astype(BF16)
+    got = dot(picks[...], wanted)
+    blocks = []
+    for ex in range(3):
+        for a in range(8):
+            blocks.append(jnp.concatenate(
+                [got[(ex * 9 + e) * 8 : (ex * 9 + e) * 8 + 8, 64 * a : 64 * a + 64] for e in range(9)], axis=1))
+    sources = jnp.concatenate(blocks, axis=0).astype(BF16)
+    total = None
+    for at in range(terms // QUAD):
+        spread = dot(sources, tables[0, :, at * 256 : at * 256 + 256]).astype(BF16)
+        part = dot(block_mix[at * 256 : at * 256 + 256, :], spread)
+        total = part if total is None else total + part
+    direct = total[:64, :64]
+    for k in range(1, QUAD):
+        direct = direct + total[64 * k : 64 * k + 64, 64 * k : 64 * k + 64]
 
     ready("mid_in", "mid_out", "own_out", "mid_nbr", "coarse_nbr")
     all_rows = rows.at[pl.ds(0, devices - 1)]
@@ -439,26 +464,6 @@
     for a in range(8):
         mid_ref[0:1, 64 * a : 64 * a + 64] = mid_out[a : a + 1]
 
-    for cell in others:
-        @pl.when(inside(steps[cell]))
-        def _(cell=cell):
-            halo_copy(26 - cell).wait_recv()
-    wanted = halo[...].astype(F32).reshape(216, 512).astype(BF16)
-    got = dot(picks[...], wanted)
-    blocks = []
-    for ex in range(3):
-        for a in range(8):
-            blocks.append(jnp.concatenate(
-                [got[(ex * 9 + e) * 8 : (ex * 9 + e) * 8 + 8, 64 * a : 64 * a + 64] for e in range(9)], axis=1))
-    sources = jnp.concatenate(blocks, axis=0).astype(BF16)
-    total = None
-    for at in range(terms // QUAD):
-        spread = dot(sources, tables[0, :, at * 256 : at * 256 + 256]).astype(BF16)
-        part = dot(block_mix[at * 256 : at * 256 + 256, :], spread)
-        total = part if total is None else total + part
-    direct = total[:64, :64]
-    for k in range(1, QUAD):
-        direct = direct + total[64 * k : 64 * k + 64, 64 * k : 64 * k + 64]
     fine = live * (direct + to_children(open_plane(mid_out)))
     fine_ref[...] = jnp.concatenate([fine[8 * x : 8 * x + 8] for x in range(8)], axis=1)
 
@@ -519,10 +524,11 @@
                dict(zip(const_names, ins[n_args:])), outs, (loaded, held) + tuple(refs[n_args + n_consts :]))
 
     vmem = pl.BlockSpec(memory_space=pltpu.VMEM)
-    hbm = pl.BlockSpec(memory_space=pl.ANY)
-    return pl.pallas_call(
+    hbm = pl.BlockSpec(memory_space=pltpu.HBM)
+    shapes = ((8, 512), (1, 512))
+    inner = pl.pallas_call(
         body,
-        out_shape=(jax.ShapeDtypeStruct((8, 512), F32), jax.ShapeDtypeStruct((1, 512), F32)),
+        out_shape=tuple(pltpu.VMEM(shape, F32) for shape in shapes),
         in_specs=[hbm] * (len(args) + len(consts)),
         out_specs=(vmem, vmem),
         scratch_shapes=scratch,
@@ -530,6 +536,26 @@
             collective_id=0, has_side_effects=True, vmem_limit_bytes=58 * 1024 * 1024),
         name="tree",
     )(*args.values(), *consts.values())
+
+    def store(fine_in, mid_in, fine_to, mid_to, sem):
+        copies = [
+            pltpu.make_async_copy(fine_in, fine_to, sem.at[0]),
+            pltpu.make_async_copy(mid_in, mid_to, sem.at[1]),
+        ]
+        for copy in copies:
+            copy.start()
+        for copy in copies:
+            copy.wait()
+
+    return pl.pallas_call(
+        store,
+        out_shape=tuple(jax.ShapeDtypeStruct(shape, F32) for shape in shapes),
+        in_specs=[pl.BlockSpec(memory_space=pl.ANY)] * 2,
+        out_specs=(hbm, hbm),
+        scratch_shapes=[dma((2,))],
+        compiler_params=pltpu.CompilerParams(vmem_limit_bytes=1 << 20),
+        name="store",
+    )(*inner)
 
 
 def solution(mesh):

time: 22.6 us -> 18.3 us (0.81)
  local copies, waits for them, and re-layouts: 2.55 us -> 0 us
  Pallas kernels: 17.8 us -> 16.2 us
    unnamed x2 -> x0, local copies, waits for them, and re-layouts: 2.55 us -> none
    pallas_call x1 -> x2, Pallas kernels: 17.8 us -> 16.2 us  [the longest x1 15.6 us: shards(): pl.pallas_call(body, out_shape=tuple((pltpu.VMEM(shape, F32) for shape in...]
where the time goes in v2:
time: 18.3 us; the launch traced here: 18.1 us
  Pallas kernels  16.2 us (89%)
  between operations  1.93 us (11%)
    pallas_call x1, Pallas kernels, shards(): pl.pallas_call(body, out_shape=tuple((pltpu.VMEM(shape, F32) for shape in...  15.6 us
    pallas_call x1, Pallas kernels, shards(): pl.pallas_call(store, out_shape=tuple((jax.ShapeDtypeStruct(shape, F32) f...  0.63 us

profile of v2, /device:TPU:0, one launch (start us, length us, event | category | flops | bytes accessed | tf_op | source)
XLA Modules:
  0.0 18.1 jit_solution(7263312683558492009)
XLA Ops:
  1.9 15.6 %tree.1 = (f32[8,512]{1,0:T(8,128)S(1)}, f32[1,512]{1,0:T(1,128)S(1)}) custom-call(s32[1,8]{1,0:T(1,128)} %refs_0_.1, s32[1]{0:T(128)S(6)} %copy.23.refs_1_, s32[1]{0:T(128)S(6)} %copy.24.refs_2_, bf16[8,512]{1,0:T(8,128)(2,1)} %refs_3_.1, bf16[1,512]{1,0:T(2,128)(2,1)} %refs_4_.1, s32[8,27]{1,0:T(8,128)} %refs_5_.1, s32[1,27]{1,0:T(1,128)} %refs_6_.1, ...), custom_call_target="tpu_custom_call" | custom-call | tf_op jit(solution)/shard_map/tree/pallas_call | solution.py:529
  17.5 0.6 %store.1 = (f32[8,512]{1,0:T(8,128)}, f32[1,512]{1,0:T(1,128)}) custom-call(f32[8,512]{1,0:T(8,128)S(1)} %get-tuple-element.4.fine_in, f32[1,512]{1,0:T(1,128)S(1)} %get-tuple-element.5.mid_in), custom_call_target="tpu_custom_call" | custom-call | tf_op jit(solution)/shard_map/store/pallas_call | solution.py:550

commit v3 on v2

v3 whole, which is shorter than its diff:
```python
import math

import jax
import jax.numpy as jnp
import numpy as np
from jax import lax
from jax.experimental import pallas as pl
from jax.experimental.pallas import tpu as pltpu
from jax.sharding import PartitionSpec as P

MESH = pl.DeviceIdType.MESH
AXES = ("gx", "gy", "gz")
CENTRE = 13
QUAD = 4
EARLY = 1
GROUPS = 4
F32 = jnp.float32
BF16 = jnp.bfloat16


def poly_multiply(left, right):
    result = [0.0] * (len(left) + len(right) - 1)
    for first, left_coef in enumerate(left):
        for second, right_coef in enumerate(right):
            result[first + second] += left_coef * right_coef
    return result


def poly_compose(coeffs, factor, offset):
    result = [0.0]
    power_term = [1.0]
    for coef in coeffs:
        padded = result + [0.0] * (len(power_term) - len(result))
        result = [padded[place] + coef * power_term[place] for place in range(len(power_term))]
        power_term = poly_multiply(power_term, [offset, factor])
    return result


def legendre_table(basis_order):
    polys = [[1.0], [0.0, 1.0]]
    for degree in range(1, basis_order):
        upper = [0.0] + [(2 * degree + 1) * coef for coef in polys[degree]]
        lower = [degree * coef for coef in polys[degree - 1]] + [0.0] * (
            len(upper) - len(polys[degree - 1])
        )
        polys.append([(upper[place] - lower[place]) / (degree + 1) for place in range(len(upper))])
    return [
        [math.sqrt(2 * degree + 1) * coef for coef in poly_compose(polys[degree], 2.0, -1.0)]
        for degree in range(basis_order)
    ]


def two_scale(basis_order):
    shifted = legendre_table(basis_order)
    filters = np.zeros((2, basis_order, basis_order))
    for which_half in range(2):
        for row_at in range(basis_order):
            halved = poly_compose(shifted[row_at], 0.5, 0.5 * which_half)
            for col_at in range(basis_order):
                product = poly_multiply(halved, shifted[col_at])
                total = sum((coef / (place + 1) for place, coef in enumerate(product)))
                filters[which_half, row_at, col_at] = total / math.sqrt(2.0)
    return np.asarray(filters, np.float32)


def halves(array):
    high = array.astype(BF16)
    return high, (array - high.astype(array.dtype)).astype(BF16)


def np_halves(array):
    array = np.asarray(array, np.float32)
    high = array.astype(BF16)
    return high, (array - high.astype(np.float32)).astype(BF16)


def dot(left, right):
    return jnp.dot(left, right, preferred_element_type=F32)


def dot_rows(left, right):
    return lax.dot_general(left, right, (((1,), (1,)), ((), ())), preferred_element_type=F32)


def constants(terms, devices, batch):
    filters = two_scale(8)
    exact = np.asarray(filters, np.float64)
    table = {}
    row = np.arange(8 * terms)
    lane = np.arange(64 * QUAD)
    same = (row % terms)[:, None] == (lane // 64)[None, :]
    spread = [same & ((row // terms)[:, None] == part[None, :]) for part in (lane // 8 % 8, lane % 8)]
    table["spread"] = np.concatenate(spread, axis=1).astype(BF16)
    swap = (row // 8)[:, None] == (row % terms)[None, :]
    swap &= (row % 8)[:, None] == (row // terms)[None, :]
    table["swap"] = swap.astype(BF16)
    table["widen"] = (np.arange(72)[:, None] == (np.arange(192) // 8)[None, :]).astype(BF16)
    close = np.einsum("jqy,lrz->jlyzqr", exact, exact).reshape(256, 64)
    opened = np.ascontiguousarray(close.T)
    twice = np.concatenate([close, close], axis=1)
    table["close"] = np.concatenate(np_halves(twice), axis=1)
    table["open"] = np.concatenate([np.concatenate(np_halves(opened), axis=1)] * 2, axis=0)
    table["coarse"] = np.concatenate(np_halves(twice) + np_halves(close @ opened), axis=1)
    fold = np.tile(np.eye(64, dtype=np.float32), (2, 2)).astype(BF16)
    stack = np.tile(opened, (2, 1))
    table["mid_tail"] = np.concatenate((fold,) + np_halves(stack), axis=1)
    tails = []
    for jl in range(4):
        mine = opened[:, 64 * jl : 64 * jl + 64]
        both = np.tile(np.concatenate([mine, mine], axis=1), (2, 1))
        tails.append(np.concatenate(np_halves(both) + np_halves(np.tile(mine @ opened, (2, 1))), axis=1))
    table["coarse_tail"] = np.stack(tails)
    parts = [np.asarray(part, np.float32) for part in np_halves(filters)]
    both = np.stack(parts, axis=1).reshape(4, 8, 8)
    flip = np.swapaxes(both, 1, 2)
    table["child_in"] = np.repeat(both, 8, axis=2)
    chains = [[exact[i].T for i in range(2)]]
    chains += [[exact[i].T @ exact[own].T for i in range(2)] for own in range(2)]
    out = np.stack([np.stack(np_halves(chain)) for chain_set in chains for chain in chain_set])
    out = np.asarray(out, np.float32).reshape(12, 8, 8)
    table["child_out"] = np.tile(np.repeat(out, 8, axis=1), (1, 1, 2))
    table["mid_in"] = np.tile(both, (1, 1, devices))
    table["mid_out"] = np.tile(flip, (1, 1, batch))
    own = [np.concatenate([flip[2 * i], flip[2 * i], flip[2 * i + 1]], axis=1) for i in range(2)]
    table["own_out"] = np.stack(own)
    cell = np.arange(27 * 8) // 8
    cells = np.zeros((8, 27 * 8), np.int32)
    cells[:4] = np.stack([cell // 9 - 1, cell // 3 % 3 - 1, cell % 3 - 1, np.arange(27 * 8) % 8])
    table["cells"] = cells
    return table


def kernel(sizes, batch, levels, terms, coarse, args, consts, outs, scratch):
    size_x, size_y, size_z = sizes
    devices = size_x * size_y * size_z
    here = [lax.axis_index(axis) for axis in AXES]
    me = (here[0] * size_y + here[1]) * size_z + here[2]
    fine_ref, mid_ref = outs
    (loaded, held, halo, rows, codes, factor_left, factor_right, tables, mixers, mixers_t, block_mix, spreads, picks,
     coarse_tab, load_sem, held_sem, row_send, row_recv, code_send, code_recv, halo_send, halo_recv) = scratch

    def each_peer(body):
        if devices <= 64:
            spots = [
                [at] + [lax.rem(at + k, size) for k in range(1, size)] for at, size in zip(here, sizes)
            ]
            peers = [(x, y, z) for x in spots[0] for y in spots[1] for z in spots[2]]
            for peer in peers[1:]:
                body(peer)
        else:
            def step(offset, carry):
                device = lax.rem(me + offset, devices)
                body((device // (size_y * size_z), device // size_z % size_y, device % size_z))
                return carry
            lax.fori_loop(1, devices, step, 0)

    loads = {}
    for at, (name, source) in enumerate(args.items()):
        loads[name] = pltpu.make_async_copy(source, loaded[name], load_sem.at[at])
    for at, (name, source) in enumerate(consts.items()):
        loads[name] = pltpu.make_async_copy(source, held[name], held_sem.at[at])
    order = ["mid_child", "mid_parent", "mid_refined", "fine_coef", "mid_leaf", "child_in", "close",
             "child_out", "open"]
    order += [name for name in loads if name not in order]
    for name in order[:9]:
        loads[name].start()
    barrier = pltpu.get_barrier_semaphore()
    each_peer(lambda peer: pl.semaphore_signal(
        barrier, inc=1, device_id=peer, device_id_type=MESH))
    for name in order[9:]:
        loads[name].start()

    def ready(*wanted):
        for name in wanted:
            loads[name].wait()

    def turn(array):
        return pltpu.roll(array, 64, 1)

    def lanes(shape):
        return lax.broadcasted_iota(jnp.int32, shape, len(shape) - 1)

    def stack_halves(array):
        high, low = halves(array)
        return jnp.concatenate([high.astype(F32), low.astype(F32)], axis=0).astype(BF16)

    def triple(array):
        high, low = halves(array)
        high, low = high.astype(F32), low.astype(F32)
        return jnp.concatenate([high, low, high], axis=0)

    half_lane = lax.shift_right_logical(lanes((8, 128)), 6)
    low_lane = half_lane == 0

    ready("mid_child", "mid_parent", "mid_refined", "fine_coef", "mid_leaf", "child_in", "close")
    child = [loaded["mid_child"][0, o] for o in range(8)]
    refined = loaded["mid_refined"][0] > 0
    live = jnp.where(refined, 1.0, 0.0).astype(F32)
    mid_parent = loaded["mid_parent"][0]
    my_parent = lax.shift_right_logical(mid_parent, 3)
    my_octant = mid_parent & 7
    code_lane = lax.shift_right_logical(lanes((2, 128)), 3) == (me & 15)
    code_row = lax.broadcasted_iota(jnp.int32, (2, 128), 0) == 1
    codes[me] = jnp.where(code_lane | code_row, mid_parent + 1, 0).astype(F32)

    flat = loaded["fine_coef"][...].astype(F32)
    by_row = []
    for k in range(4):
        tile = flat[:, 128 * k : 128 * k + 128]
        turned = turn(tile)
        by_row += [jnp.where(low_lane, tile, turned), jnp.where(low_lane, turned, tile)]
    by_row = jnp.concatenate(by_row, axis=0)
    slot_lane = lanes((8, 64)) & 7
    child_in = [held["child_in"][k] for k in range(4)]
    blocks = []
    for part in range(2):
        for jl in range(4):
            block = jnp.where(slot_lane == child[jl], child_in[part], 0.0)
            blocks.append(block + jnp.where(slot_lane == child[4 + jl], child_in[2 + part], 0.0))
    mixed = dot(jnp.concatenate(blocks, axis=0).astype(BF16), by_row.astype(BF16))
    mixed = mixed[:32] + mixed[32:]
    wide = [jnp.where(low_lane, mixed[16 * j : 16 * j + 8], mixed[16 * j + 8 : 16 * j + 16]) for j in range(2)]
    got = dot(stack_halves(jnp.concatenate(wide, axis=1)), held["close"][...])
    compressed = got[:8, :128] + got[:8, 128:] + got[8:, :128]
    leaf = jnp.broadcast_to(loaded["mid_leaf"][...].astype(F32), (8, 512))
    leaf_block = lax.shift_right_logical(lanes((8, 512)), 6)
    leaf = jnp.where(leaf_block == lax.broadcasted_iota(jnp.int32, (8, 512), 0), leaf, 0.0)
    leaf = leaf[:, :128] + leaf[:, 128:256] + leaf[:, 256:384] + leaf[:, 384:]
    leaf = leaf + turn(leaf)
    mid_source = jnp.where(refined, compressed, leaf)
    placed = jnp.where(half_lane == (my_octant & 1), mid_source, 0.0).astype(BF16)
    rows[me] = placed

    ready("child_out", "open")
    j_lane = lax.shift_right_logical(lanes((64, 16)), 3)
    slot_row = lax.broadcasted_iota(jnp.int32, (64, 16), 0) & 7
    chosen = []
    for i in range(2):
        ends = [jnp.where(j_lane == 0, child[4 * i + l], child[4 * i + 2 + l]) for l in range(2)]
        chosen.append((slot_row == ends[0]) | (slot_row == ends[1]))

    def child_matrix(at):
        parts = [
            jnp.where(chosen[0], held["child_out"][4 * at + part], 0.0)
            + jnp.where(chosen[1], held["child_out"][4 * at + 2 + part], 0.0)
            for part in range(2)
        ]
        return [parts[0], parts[0], parts[1]]

    odd = lax.broadcasted_iota(jnp.int32, (8, 128), 0)
    odd = (odd == child[1]) | (odd == child[3]) | (odd == child[5]) | (odd == child[7])
    child_half = jnp.concatenate([odd == (half_lane == 1)] * 8, axis=0)

    def j_rows(plane):
        return jnp.concatenate([plane[:, :128], plane[:, 128:]], axis=0)

    def settle(array):
        array = jnp.where(child_half, array, 0.0)
        return array + turn(array)

    def to_flat(array):
        pairs = [jnp.where(low_lane, array[16 * k : 16 * k + 8], array[16 * k + 8 : 16 * k + 16]) for k in range(4)]
        return jnp.concatenate(pairs, axis=1)

    steps = [(c // 9 - 1, c // 3 % 3 - 1, c % 3 - 1) for c in range(27)]

    def inside(step):
        tests = []
        for at, size, move in zip(here, sizes, step):
            if move == 1:
                tests.append(at < size - 1)
            elif move == -1:
                tests.append(at > 0)
        found = tests[0]
        for test in tests[1:]:
            found = found & test
        return found

    def halo_copy(cell):
        peer = tuple(at + part for at, part in zip(here, steps[cell]))
        return pltpu.make_async_remote_copy(
            src_ref=halo.at[CENTRE],
            dst_ref=halo.at[26 - cell],
            send_sem=halo_send.at[cell],
            recv_sem=halo_recv.at[26 - cell],
            device_id=peer,
            device_id_type=MESH,
        )

    def to_all(buffer, send, recv):
        each_peer(lambda peer: pltpu.make_async_remote_copy(
            src_ref=buffer.at[me],
            dst_ref=buffer.at[me],
            send_sem=send.at[0],
            recv_sem=recv.at[0],
            device_id=peer,
            device_id_type=MESH,
        ).start())

    others = [cell for cell in range(27) if cell != CENTRE]

    def meet_and_send():
        pl.semaphore_wait(barrier, devices - 1)
        to_all(codes, code_send, code_recv)
        to_all(rows, row_send, row_recv)

    def build_tables():
        ready("op_factor", "term_weight", "spread", "swap", "widen")
        factor = loaded["op_factor"]
        planes = []
        for level in range(levels):
            for e in range(3):
                planes.append(jnp.concatenate([factor[level, e, b] for b in range(8)], axis=1))
        plane = jnp.concatenate(planes, axis=0)
        weight = jnp.concatenate([loaded["term_weight"][...]] * 8, axis=1)
        rounded = plane.astype(BF16)
        left_side = stack_halves(plane * weight).astype(F32)
        right_side = stack_halves(plane).astype(F32)
        count = plane.shape[0]
        group = 64 * QUAD
        for at in range(terms // QUAD):
            for side, first, factors in ((left_side, 0, factor_left), (right_side, group, factor_right)):
                some = pltpu.roll(side, 8 * terms - QUAD * at, 1) if at else side
                got = dot(some.astype(BF16), held["spread"][:, first : first + group])
                got = got[:count] + got[count:]
                factors[:, :, at * group : at * group + group] = got.reshape(levels * 3, 8, group)
        turned = dot_rows(held["swap"][...], rounded)
        for level in range(1, levels):
            parts = [turned[32 * at : 32 * at + 32, 24 * level : 24 * level + 24] for at in range(terms // QUAD)]
            mixers[level - 1] = jnp.concatenate(parts, axis=1).astype(BF16)
        mixers_t[...] = dot(turned.astype(BF16), held["widen"][...])

        def table_step(at, carry):
            level, ey = at // 3, at % 3
            left = factor_left.at[at]
            for ez in range(3):
                right = factor_right[level * 3 + ez]
                base = (ey * 3 + ez) * 64
                for k in range(4):
                    pair = [left[2 * k + half : 2 * k + half + 1, :] * right for half in range(2)]
                    start = pl.multiple_of(base + 16 * k, 16)
                    tables[level, pl.ds(start, 16), :] = jnp.concatenate(pair, axis=0).astype(BF16)
            return carry

        lax.fori_loop(0, levels * 3, table_step, 0)
        own_lane = (lanes((8, 192)) & 7) == lax.broadcasted_iota(jnp.int32, (8, 192), 0)

        for at in range(terms // 2):
            some = mixers_t[16 * at : 16 * at + 16, :]
            some = jnp.where(own_lane[None], jnp.broadcast_to(some[:, None, :], (16, 8, 192)), 0.0)
            part, first, lane = at // (2 * GROUPS), 128 * (at % 2), 192 * (at // 2 % GROUPS)
            block_mix[part, first : first + 128, lane : lane + 192] = some.reshape(128, 192).astype(BF16)

    away = lax.shift_right_logical(here[0], 1) + here[1] + here[2]
    far = 2 * away > (size_x - 1) // 2 + size_y + size_z - 2
    near_start = away <= EARLY

    @pl.when(far)
    def _():
        meet_and_send()

    own_matrix = child_matrix(0)
    plane = dot(placed, held["open"][...])
    plane = plane[:, :256] + plane[:, 256:]
    fine_from = dot(jnp.concatenate(own_matrix, axis=1).astype(BF16), triple(j_rows(plane)).astype(BF16))
    detail = live * (by_row - settle(fine_from))
    halo[CENTRE] = to_flat(detail).astype(BF16)

    for cell in others:
        @pl.when(jnp.logical_not(inside(steps[cell])))
        def _(cell=cell):
            halo[cell] = jnp.zeros(halo.shape[1:], BF16)

    @pl.when(near_start)
    def _():
        build_tables()

    @pl.when(jnp.logical_not(far))
    def _():
        meet_and_send()

    for cell in others:
        @pl.when(inside(steps[cell]))
        def _(cell=cell):
            halo_copy(cell).start()

    @pl.when(jnp.logical_not(near_start))
    def _():
        build_tables()

    ready("cells", "fine_nbr")
    cells = held["cells"]
    spot = [here[k] + cells[k : k + 1, :] for k in range(3)]
    there = None
    for k in range(3):
        test = (spot[k] >= 0) & (spot[k] < sizes[k])
        there = test if there is None else there & test
    names_row = ((spot[0] * size_y + spot[1]) * size_z + spot[2]) * 8 + cells[3:4, :]
    names_row = jnp.where(there, names_row, -2)
    near = loaded["fine_nbr"][...]
    hot = [(near[:, d : d + 1] == names_row).astype(F32) for d in range(27)]
    picks[...] = jnp.concatenate(hot, axis=0).astype(BF16)

    ready("mid_in", "mid_out", "own_out", "mid_nbr", "coarse_nbr", "coarse", "mid_tail", "coarse_tail")
    after_matrix = [jnp.where(my_octant >= 4, upper, lower)
                    for lower, upper in zip(child_matrix(1), child_matrix(2))]
    last_matrix = jnp.concatenate(own_matrix + after_matrix, axis=1).astype(BF16)
    own_out = jnp.where(my_octant >= 4, held["own_out"][1], held["own_out"][0]).astype(BF16)

    def arrived(buffer, sem):
        span = buffer.at[pl.ds(0, devices - 1)]
        return pltpu.make_async_copy(span, span, sem.at[0])

    arrived(codes, code_recv).wait()
    code = [
        jnp.sum(codes[first : min(first + 16, devices)], axis=0)[0:1] for first in range(0, devices, 16)
    ]
    code = jnp.concatenate(code, axis=1)[:, : devices * 8].astype(jnp.int32) - 1
    key = lax.shift_right_arithmetic(jnp.broadcast_to(code, (8, devices * 8)), 1)
    near_id = [loaded["mid_nbr"][0, d] for d in range(27)]
    near_code = []
    for named in near_id:
        got = codes[jnp.maximum(named, 0)][1:2, :].astype(jnp.int32)
        near_code.append(jnp.broadcast_to(jnp.where(named >= 0, got, 0) - 1, (8, 128)))
    batch_lane = lax.shift_right_logical(lanes((8, batch * 8)), 3)

    def choose_in(first):
        blocks = []
        for part in range(2):
            for k in range(batch):
                for j in range(2):
                    want = (first + k) * 4 + j
                    block = jnp.where(key == want, held["mid_in"][part], 0.0)
                    blocks.append(block + jnp.where(key == want + 2, held["mid_in"][2 + part], 0.0))
        return jnp.concatenate(blocks, axis=0).astype(BF16)

    def choose_out(first):
        lane_key = (first + batch_lane) * 2
        parts = [[], []]
        for d in range(27):
            mine = lax.shift_right_arithmetic(near_code[d][:, : batch * 8], 2)
            lower, upper = mine == lane_key, mine == lane_key + 1
            for part in range(2):
                block = jnp.where(lower, held["mid_out"][part], 0.0)
                parts[part].append(block + jnp.where(upper, held["mid_out"][2 + part], 0.0))
        parts = [jnp.concatenate(part, axis=0) for part in parts]
        return jnp.concatenate([parts[0], parts[0], parts[1]], axis=1).astype(BF16)

    batches = coarse // batch
    if batches == 1:
        first_in, first_out = choose_in(0), choose_out(0)

    for cell in others:
        @pl.when(inside(steps[cell]))
        def _(cell=cell):
            halo_copy(26 - cell).wait_recv()
    got = dot(picks[...], halo[...].astype(F32).reshape(216, 512).astype(BF16))
    blocks = []
    for ex in range(3):
        here_rows = [got[(ex * 9 + e) * 8 : (ex * 9 + e) * 8 + 8] for e in range(9)]
        for k in range(4):
            tile = [part[:, 128 * k : 128 * k + 128] for part in here_rows]
            turned = [turn(part) for part in tile]
            even = [jnp.where(low_lane, tile[e], turned[e + 1]) for e in range(0, 8, 2)]
            uneven = [jnp.where(low_lane, turned[e], tile[e + 1]) for e in range(0, 8, 2)]
            blocks.append(jnp.concatenate(even + [tile[8][:, :64]], axis=1))
            blocks.append(jnp.concatenate(uneven + [turned[8][:, :64]], axis=1))
    fine_sources = jnp.concatenate(blocks, axis=0).astype(BF16)
    fine_total = []

    def spread_fine(at):
        spread = dot(fine_sources, tables[0, :, at * 256 : at * 256 + 256])
        spreads[192 * at : 192 * at + 192, :] = spread.astype(BF16)

    def mix_fine(part):
        rows_of = 192 * GROUPS
        fine_total.append(dot(block_mix[part], spreads[rows_of * part : rows_of * part + rows_of, :]))

    fine_work = []
    for at in range(terms // QUAD):
        fine_work.append(lambda at=at: spread_fine(at))
        if at >= GROUPS and at % GROUPS == 0:
            fine_work.append(lambda part=at // GROUPS - 1: mix_fine(part))
    fine_work.append(lambda: mix_fine(terms // QUAD // GROUPS - 1))
    fine_work = iter(fine_work)

    def fine_step(count=1):
        for _, work in zip(range(count), fine_work):
            work()

    arrived(rows, row_recv).wait()
    gathered = rows[...].astype(F32).reshape(devices * 8, 128).astype(BF16)

    def coarse_step(at, total, chosen_in, chosen_out, between=lambda: None):
        mixed = dot(chosen_in, gathered)
        between()
        mixed = mixed[: batch * 16] + mixed[batch * 16 :]
        wide = [
            jnp.concatenate([mixed[16 * k : 16 * k + 8], mixed[16 * k + 8 : 16 * k + 16]], axis=1)
            for k in range(batch)
        ]
        got = dot(stack_halves(jnp.concatenate(wide, axis=0)), held["coarse"][...])
        between()
        top = batch * 8
        plane = got[:top, 256:512] + got[:top, 512:] + got[top:, 256:512]
        source = got[:top, :128] + got[:top, 128:256] + got[top:, :128]
        coarse_tab[pl.ds(at * batch, batch)] = source.reshape(batch, 8, 128)
        found = dot(chosen_out, triple(plane).astype(BF16))
        return found if total is None else total + found

    zero = jnp.zeros((216, 256), F32)
    if batches == 1:
        from_coarse = coarse_step(0, None, first_in, first_out, fine_step)
    else:
        from_coarse = lax.fori_loop(
            0, batches,
            lambda at, total: coarse_step(at, total, choose_in(at * batch), choose_out(at * batch)), zero)

    def pair_up(blocks):
        pairs = [jnp.where(low_lane, blocks[e], blocks[e + 1]) for e in range(0, 8, 2)]
        return jnp.concatenate(pairs + [blocks[8][:, :64]], axis=1)

    coarse_blocks = []
    for ex in range(3):
        got = []
        for e in range(9):
            named = loaded["coarse_nbr"][my_parent, ex * 9 + e]
            got.append(jnp.where(named >= 0, coarse_tab[jnp.maximum(named, 0)], 0.0))
        coarse_blocks.append(pair_up(got))
    coarse_sources = jnp.concatenate(coarse_blocks, axis=0).astype(BF16)
    quad_lane = lax.shift_right_logical(lanes((8, 256)), 6)

    def spread_one(level, sources):
        return dot(sources, tables[level])

    def mix_one(level, spread):
        parts = [spread[:, at * 256 : at * 256 + 256] for at in range(terms // QUAD)]
        total = dot(mixers[level - 1], jnp.concatenate(parts, axis=0).astype(BF16))
        fine_step()
        result = jnp.where(quad_lane == 0, total[:8], 0.0)
        for k in range(1, QUAD):
            result = jnp.where(quad_lane == k, total[8 * k : 8 * k + 8], result)
        return result[:, :128] + result[:, 128:]

    coarse_spread = spread_one(2, coarse_sources)
    near_blocks = []
    for d in range(27):
        tile = jnp.where(near_id[d] >= 0, rows[jnp.maximum(near_id[d], 0)].astype(F32), 0.0)
        part = from_coarse[8 * d : 8 * d + 8]
        part = jnp.where((near_code[d] & 2) > 0, part[:, 128:], part[:, :128])
        tile = tile - jnp.where(half_lane == (near_code[d] & 1), part, 0.0)
        near_blocks.append(tile + turn(tile))
    mid_sources = [pair_up(near_blocks[9 * ex : 9 * ex + 9]) for ex in range(3)]
    mid_sources = jnp.concatenate(mid_sources, axis=0).astype(BF16)
    mid_spread = spread_one(1, mid_sources)
    coarse_raw = mix_one(2, coarse_spread)
    tail = dot(stack_halves(coarse_raw), held["coarse_tail"][my_octant & 3])
    fine_step()
    mid_raw = mix_one(1, mid_spread)
    got = tail
    mine = got[:8, :128] + got[:8, 128:256] + got[8:, :128]
    coarse_plane = got[:8, 256:512] + got[:8, 512:] + got[8:, 256:512]
    tail = dot(stack_halves(mid_raw), held["mid_tail"][...])
    from_above = dot(own_out, triple(mine).astype(BF16))
    fine_step()
    got = tail
    mid_plane = got[:8, 128:384] + got[:8, 384:] + got[8:, 128:384]
    planes = jnp.concatenate([triple(j_rows(mid_plane)), triple(j_rows(coarse_plane))], axis=0)
    fine_from = dot(last_matrix, planes.astype(BF16))
    fine_step(3 * terms)
    fine_from = settle(fine_from)
    mid_out = got[:8, :128] + got[8:, :128] + from_above
    for a in range(8):
        at = 64 * (a % 2)
        mid_ref[0:1, 64 * a : 64 * a + 64] = mid_out[a : a + 1, at : at + 64]

    total = sum(fine_total[1:], fine_total[0])
    direct = []
    for a in range(8):
        part = jnp.where(quad_lane == 0, total[8 * a : 8 * a + 8], 0.0)
        for k in range(1, QUAD):
            part = jnp.where(quad_lane == k, total[64 * k + 8 * a : 64 * k + 8 * a + 8], part)
        direct.append(part[:, :128] + part[:, 128:])
    direct = jnp.concatenate(direct, axis=0)
    direct = direct + turn(direct)
    fine_ref[...] = to_flat(live * (direct + fine_from))

    arrived(codes, code_send).wait()
    arrived(rows, row_send).wait()
    for cell in others:
        @pl.when(inside(steps[cell]))
        def _(cell=cell):
            halo_copy(cell).wait_send()


SCALARS = ("mid_child", "mid_parent", "mid_refined", "mid_nbr", "coarse_nbr")


def shards(sizes, fine_coef, mid_leaf, mid_child, mid_parent, mid_refined, fine_nbr, mid_nbr, coarse_nbr,
           op_factor, term_weight):
    levels, terms = op_factor.shape[:2]
    coarse = coarse_nbr.shape[0]
    devices = math.prod(sizes)
    batch = math.gcd(coarse, 4)
    assert mid_child.shape == (1, 8) and fine_coef.shape == (8, 512) and terms % QUAD == 0
    args = dict(
        mid_child=mid_child, mid_parent=mid_parent, mid_refined=mid_refined, fine_coef=fine_coef,
        mid_leaf=mid_leaf, fine_nbr=fine_nbr, mid_nbr=mid_nbr, coarse_nbr=coarse_nbr,
        op_factor=jnp.transpose(op_factor, (0, 2, 3, 4, 1)), term_weight=term_weight[None, :],
    )
    consts = {name: jnp.asarray(value) for name, value in constants(terms, devices, batch).items()}
    arg_names, const_names = list(args), list(consts)
    dma = pltpu.SemaphoreType.DMA
    width = 64 * terms

    def buffer(name, value):
        space = pltpu.SMEM if name in SCALARS else pltpu.VMEM
        return space(value.shape, value.dtype)

    scratch = [buffer(name, value) for name, value in args.items()]
    scratch += [buffer(name, value) for name, value in consts.items()]
    scratch += [
        pltpu.VMEM((27, 8, 512), BF16),
        pltpu.VMEM((devices, 8, 128), BF16),
        pltpu.VMEM((devices, 2, 128), F32),
        pltpu.VMEM((levels * 3, 8, width), F32),
        pltpu.VMEM((levels * 3, 8, width), F32),
        pltpu.VMEM((levels, 576, width), BF16),
        pltpu.VMEM((levels - 1, 8 * QUAD, 24 * (terms // QUAD)), BF16),
        pltpu.VMEM((8 * terms, 192), F32),
        pltpu.VMEM((terms // QUAD // GROUPS, 64 * QUAD, 192 * GROUPS), BF16),
        pltpu.VMEM((192 * (terms // QUAD), 64 * QUAD), BF16),
        pltpu.VMEM((216, 216), BF16),
        pltpu.VMEM((coarse, 8, 128), F32),
        dma((len(args),)), dma((len(consts),)), dma((1,)), dma((1,)), dma((1,)), dma((1,)), dma((27,)), dma((27,)),
    ]

    def body(*refs):
        n_args, n_consts = len(arg_names), len(const_names)
        ins, refs = refs[: n_args + n_consts], refs[n_args + n_consts :]
        outs, refs = refs[:2], refs[2:]
        loaded = dict(zip(arg_names, refs[:n_args]))
        held = dict(zip(const_names, refs[n_args : n_args + n_consts]))
        kernel(sizes, batch, levels, terms, coarse, dict(zip(arg_names, ins[:n_args])),
               dict(zip(const_names, ins[n_args:])), outs, (loaded, held) + tuple(refs[n_args + n_consts :]))

    vmem = pl.BlockSpec(memory_space=pltpu.VMEM)
    hbm = pl.BlockSpec(memory_space=pltpu.HBM)
    shapes = ((8, 512), (1, 512))
    inner = pl.pallas_call(
        body,
        out_shape=tuple(pltpu.VMEM(shape, F32) for shape in shapes),
        in_specs=[hbm] * (len(args) + len(consts)),
        out_specs=(vmem, vmem),
        scratch_shapes=scratch,
        compiler_params=pltpu.CompilerParams(
            collective_id=0, has_side_effects=True, vmem_limit_bytes=58 * 1024 * 1024),
        name="tree",
    )(*args.values(), *consts.values())

    def store(fine_in, mid_in, fine_to, mid_to, sem):
        copies = [
            pltpu.make_async_copy(fine_in, fine_to, sem.at[0]),
            pltpu.make_async_copy(mid_in, mid_to, sem.at[1]),
        ]
        for copy in copies:
            copy.start()
        for copy in copies:
            copy.wait()

    return pl.pallas_call(
        store,
        out_shape=tuple(jax.ShapeDtypeStruct(shape, F32) for shape in shapes),
        in_specs=[pl.BlockSpec(memory_space=pl.ANY)] * 2,
        out_specs=(hbm, hbm),
        scratch_shapes=[dma((2,))],
        compiler_params=pltpu.CompilerParams(vmem_limit_bytes=1 << 20),
        name="store",
    )(*inner)


def solution(mesh):
    sizes = tuple(mesh.shape[axis] for axis in AXES)
    split = P(AXES, None)
    line = P(AXES)
    return jax.shard_map(
        lambda *args: shards(sizes, *args),
        mesh=mesh,
        in_specs=(split, split, split, line, line, split, split, P(), P(), P()),
        out_specs=(split, split),
        check_vma=False,
    )
```

time: 18.3 us -> 17 us (0.929)
  Pallas kernels: 16.2 us -> 14.9 us
    pallas_call x1, Pallas kernels: 15.6 us -> 14.3 us  [shards(): pl.pallas_call(body, out_shape=tuple((pltpu.VMEM(shape, F32) for shape in...]
where the time goes in v3:
time: 17 us; the launch traced here: 16.9 us
  Pallas kernels  14.9 us (88%)
  between operations  1.93 us (11%)
    pallas_call x1, Pallas kernels, shards(): pl.pallas_call(body, out_shape=tuple((pltpu.VMEM(shape, F32) for shape in...  14.3 us
    pallas_call x1, Pallas kernels, shards(): pl.pallas_call(store, out_shape=tuple((jax.ShapeDtypeStruct(shape, F32) f...  0.63 us

profile of v3, /device:TPU:0, one launch (start us, length us, event | category | flops | bytes accessed | tf_op | source)
XLA Modules:
  0.0 16.9 jit_solution(9822448439349627195)
XLA Ops:
  1.9 14.3 %tree.1 = (f32[8,512]{1,0:T(8,128)S(1)}, f32[1,512]{1,0:T(1,128)S(1)}) custom-call(s32[1,8]{1,0:T(1,128)} %refs_0_.1, s32[1]{0:T(128)S(6)} %copy.26.refs_1_, s32[1]{0:T(128)S(6)} %copy.27.refs_2_, bf16[8,512]{1,0:T(8,128)(2,1)} %refs_3_.1, bf16[1,512]{1,0:T(2,128)(2,1)} %refs_4_.1, s32[8,27]{1,0:T(8,128)} %refs_5_.1, s32[1,27]{1,0:T(1,128)} %refs_6_.1, ...), custom_call_target="tpu_custom_call" | custom-call | tf_op jit(solution)/shard_map/tree/pallas_call | solution.py:650
  16.2 0.6 %store.1 = (f32[8,512]{1,0:T(8,128)}, f32[1,512]{1,0:T(1,128)}) custom-call(f32[8,512]{1,0:T(8,128)S(1)} %get-tuple-element.4.fine_in, f32[1,512]{1,0:T(1,128)S(1)} %get-tuple-element.5.mid_in), custom_call_target="tpu_custom_call" | custom-call | tf_op jit(solution)/shard_map/store/pallas_call | solution.py:671

commit v4 on v3

--- a/solution.py
+++ b/solution.py
@@ -139,14 +139,17 @@
     (loaded, held, halo, rows, codes, factor_left, factor_right, tables, mixers, mixers_t, block_mix, spreads, picks,
      coarse_tab, load_sem, held_sem, row_send, row_recv, code_send, code_recv, halo_send, halo_recv) = scratch
 
-    def each_peer(body):
-        if devices <= 64:
-            spots = [
-                [at] + [lax.rem(at + k, size) for k in range(1, size)] for at, size in zip(here, sizes)
-            ]
-            peers = [(x, y, z) for x in spots[0] for y in spots[1] for z in spots[2]]
-            for peer in peers[1:]:
-                body(peer)
+    spots = [(x, y, z) for x in range(size_x) for y in range(size_y) for z in range(size_z)]
+    spots.sort(key=lambda spot: spot[0] // 2 + spot[1] + spot[2])
+    front = [spot for spot in spots if spot[0] // 2 + spot[1] + spot[2] <= EARLY]
+    unrolled = devices <= 64
+
+    def each_peer(body, chosen=spots):
+        if unrolled:
+            for spot in chosen:
+                @pl.when(me != (spot[0] * size_y + spot[1]) * size_z + spot[2])
+                def _(spot=spot):
+                    body(spot)
         else:
             def step(offset, carry):
                 device = lax.rem(me + offset, devices)
@@ -287,22 +290,40 @@
             device_id_type=MESH,
         )
 
-    def to_all(buffer, send, recv):
-        each_peer(lambda peer: pltpu.make_async_remote_copy(
-            src_ref=buffer.at[me],
-            dst_ref=buffer.at[me],
-            send_sem=send.at[0],
-            recv_sem=recv.at[0],
+    def send_code(peer):
+        pltpu.make_async_remote_copy(
+            src_ref=codes.at[me],
+            dst_ref=codes.at[me],
+            send_sem=code_send.at[0],
+            recv_sem=code_recv.at[0],
             device_id=peer,
             device_id_type=MESH,
-        ).start())
+        ).start()
+
+    def send_row(peer):
+        pltpu.make_async_remote_copy(
+            src_ref=rows.at[me],
+            dst_ref=rows.at[me],
+            send_sem=row_send.at[0],
+            recv_sem=row_recv.at[0],
+            device_id=peer,
+            device_id_type=MESH,
+        ).start()
+
+    def send_both(peer):
+        send_code(peer)
+        send_row(peer)
 
     others = [cell for cell in range(27) if cell != CENTRE]
 
     def meet_and_send():
         pl.semaphore_wait(barrier, devices - 1)
-        to_all(codes, code_send, code_recv)
-        to_all(rows, row_send, row_recv)
+        if unrolled:
+            each_peer(send_both, front)
+            each_peer(send_code, spots[len(front) :])
+            each_peer(send_row, spots[len(front) :])
+        else:
+            each_peer(send_both)
 
     def build_tables():
         ready("op_factor", "term_weight", "spread", "swap", "widen")

time: 17 us -> 16.8 us (0.988)
  Pallas kernels: 14.9 us -> 14.7 us
    pallas_call x1, Pallas kernels: 14.3 us -> 14.1 us  [shards(): pl.pallas_call(body, out_shape=tuple((pltpu.VMEM(shape, F32) for shape in...]
where the time goes in v4:
time: 16.8 us; the launch traced here: 16.7 us
  Pallas kernels  14.7 us (88%)
  between operations  1.93 us (11%)
    pallas_call x1, Pallas kernels, shards(): pl.pallas_call(body, out_shape=tuple((pltpu.VMEM(shape, F32) for shape in...  14.1 us
    pallas_call x1, Pallas kernels, shards(): pl.pallas_call(store, out_shape=tuple((jax.ShapeDtypeStruct(shape, F32) f...  0.63 us

profile of v4, /device:TPU:0, one launch (start us, length us, event | category | flops | bytes accessed | tf_op | source)
XLA Modules:
  0.0 16.7 jit_solution(32860197480019261)
XLA Ops:
  1.9 14.1 %tree.1 = (f32[8,512]{1,0:T(8,128)S(1)}, f32[1,512]{1,0:T(1,128)S(1)}) custom-call(s32[1,8]{1,0:T(1,128)} %refs_0_.1, s32[1]{0:T(128)S(6)} %copy.26.refs_1_, s32[1]{0:T(128)S(6)} %copy.27.refs_2_, bf16[8,512]{1,0:T(8,128)(2,1)} %refs_3_.1, bf16[1,512]{1,0:T(2,128)(2,1)} %refs_4_.1, s32[8,27]{1,0:T(8,128)} %refs_5_.1, s32[1,27]{1,0:T(1,128)} %refs_6_.1, ...), custom_call_target="tpu_custom_call" | custom-call | tf_op jit(solution)/shard_map/tree/pallas_call | solution.py:671
  16.0 0.6 %store.1 = (f32[8,512]{1,0:T(8,128)}, f32[1,512]{1,0:T(1,128)}) custom-call(f32[8,512]{1,0:T(8,128)S(1)} %get-tuple-element.4.fine_in, f32[1,512]{1,0:T(1,128)S(1)} %get-tuple-element.5.mid_in), custom_call_target="tpu_custom_call" | custom-call | tf_op jit(solution)/shard_map/store/pallas_call | solution.py:692

commit v5 on v4

--- a/solution.py
+++ b/solution.py
@@ -141,7 +141,7 @@
 
     spots = [(x, y, z) for x in range(size_x) for y in range(size_y) for z in range(size_z)]
     spots.sort(key=lambda spot: spot[0] // 2 + spot[1] + spot[2])
-    front = [spot for spot in spots if spot[0] // 2 + spot[1] + spot[2] <= EARLY]
+    front = [spot for spot in spots if spot[0] // 2 + spot[1] + spot[2] <= 0]
     unrolled = devices <= 64
 
     def each_peer(body, chosen=spots):
@@ -202,9 +202,8 @@
     mid_parent = loaded["mid_parent"][0]
     my_parent = lax.shift_right_logical(mid_parent, 3)
     my_octant = mid_parent & 7
-    code_lane = lax.shift_right_logical(lanes((2, 128)), 3) == (me & 15)
-    code_row = lax.broadcasted_iota(jnp.int32, (2, 128), 0) == 1
-    codes[me] = jnp.where(code_lane | code_row, mid_parent + 1, 0).astype(F32)
+    code_lane = lax.shift_right_logical(lanes((1, 128)), 3) == (me & 15)
+    codes[me] = jnp.where(code_lane, mid_parent + 1, 0).astype(F32)
 
     flat = loaded["fine_coef"][...].astype(F32)
     by_row = []
@@ -434,14 +433,14 @@
 
     arrived(codes, code_recv).wait()
     code = [
-        jnp.sum(codes[first : min(first + 16, devices)], axis=0)[0:1] for first in range(0, devices, 16)
+        jnp.sum(codes[first : min(first + 16, devices)], axis=0) for first in range(0, devices, 16)
     ]
     code = jnp.concatenate(code, axis=1)[:, : devices * 8].astype(jnp.int32) - 1
     key = lax.shift_right_arithmetic(jnp.broadcast_to(code, (8, devices * 8)), 1)
     near_id = [loaded["mid_nbr"][0, d] for d in range(27)]
     near_code = []
     for named in near_id:
-        got = codes[jnp.maximum(named, 0)][1:2, :].astype(jnp.int32)
+        got = jnp.max(codes[jnp.maximum(named, 0)], axis=1, keepdims=True).astype(jnp.int32)
         near_code.append(jnp.broadcast_to(jnp.where(named >= 0, got, 0) - 1, (8, 128)))
     batch_lane = lax.shift_right_logical(lanes((8, batch * 8)), 3)
 
@@ -643,7 +642,7 @@
     scratch += [
         pltpu.VMEM((27, 8, 512), BF16),
         pltpu.VMEM((devices, 8, 128), BF16),
-        pltpu.VMEM((devices, 2, 128), F32),
+        pltpu.VMEM((devices, 1, 128), F32),
         pltpu.VMEM((levels * 3, 8, width), F32),
         pltpu.VMEM((levels * 3, 8, width), F32),
         pltpu.VMEM((levels, 576, width), BF16),

time: 16.8 us -> 16.6 us (0.988)
  Pallas kernels: 14.7 us -> 14.5 us
    pallas_call x1, Pallas kernels: 14.1 us -> 13.9 us  [shards(): pl.pallas_call(body, out_shape=tuple((pltpu.VMEM(shape, F32) for shape in...]
where the time goes in v5:
time: 16.6 us; the launch traced here: 16.4 us
  Pallas kernels  14.5 us (87%)
  between operations  1.93 us (12%)
    pallas_call x1, Pallas kernels, shards(): pl.pallas_call(body, out_shape=tuple((pltpu.VMEM(shape, F32) for shape in...  13.9 us
    pallas_call x1, Pallas kernels, shards(): pl.pallas_call(store, out_shape=tuple((jax.ShapeDtypeStruct(shape, F32) f...  0.63 us

profile of v5, /device:TPU:0, one launch (start us, length us, event | category | flops | bytes accessed | tf_op | source)
XLA Modules:
  0.0 16.4 jit_solution(9686140450248688448)
XLA Ops:
  1.9 13.9 %tree.1 = (f32[8,512]{1,0:T(8,128)S(1)}, f32[1,512]{1,0:T(1,128)S(1)}) custom-call(s32[1,8]{1,0:T(1,128)} %refs_0_.1, s32[1]{0:T(128)S(6)} %copy.26.refs_1_, s32[1]{0:T(128)S(6)} %copy.27.refs_2_, bf16[8,512]{1,0:T(8,128)(2,1)} %refs_3_.1, bf16[1,512]{1,0:T(2,128)(2,1)} %refs_4_.1, s32[8,27]{1,0:T(8,128)} %refs_5_.1, s32[1,27]{1,0:T(1,128)} %refs_6_.1, ...), custom_call_target="tpu_custom_call" | custom-call | tf_op jit(solution)/shard_map/tree/pallas_call | solution.py:670
  15.8 0.6 %store.1 = (f32[8,512]{1,0:T(8,128)}, f32[1,512]{1,0:T(1,128)}) custom-call(f32[8,512]{1,0:T(8,128)S(1)} %get-tuple-element.4.fine_in, f32[1,512]{1,0:T(1,128)S(1)} %get-tuple-element.5.mid_in), custom_call_target="tpu_custom_call" | custom-call | tf_op jit(solution)/shard_map/store/pallas_call | solution.py:691
